TPU v7x, 32 devices: a whole 2x2x4 slice. The times are simulated.
32 devices in a mesh: ctx: 8 (over y, x, core), tp: 4 (over z).
Axes of the slice: x: 2, y: 2, z: 4, core: 2. Of those that a mesh axis runs over, the one named last changes fastest.
Arguments:
- tokens: bfloat16 [2, 1024, 2048], P(None, 'ctx', 'tp'), may hold values from -6 to 6
- w_query: bfloat16 [2048, 2048], P('ctx', 'tp'), may hold values from -0.125 to 0.125
- w_key: bfloat16 [2048, 2048], P('ctx', 'tp'), may hold values from -0.125 to 0.125
- w_value: bfloat16 [2048, 2048], P('ctx', 'tp'), may hold values from -0.125 to 0.125
- w_output: bfloat16 [2048, 2048], P('tp', 'ctx'), may hold values from -0.125 to 0.125
- w_gate: bfloat16 [2048, 8192], P('ctx', 'tp'), may hold values from -0.125 to 0.125
- w_up: bfloat16 [2048, 8192], P('ctx', 'tp'), may hold values from -0.125 to 0.125
- w_down: bfloat16 [8192, 2048], P('tp', 'ctx'), may hold values from -0.0625 to 0.0625
- gain_query: bfloat16 [2048], P(('tp', 'ctx')), may hold values from 0.5 to 1.5
- gain_key: bfloat16 [2048], P(('tp', 'ctx')), may hold values from 0.5 to 1.5
- gain_attention: bfloat16 [2048], P(('tp', 'ctx')), may hold values from 0.5 to 1.5
- gain_feedforward: bfloat16 [2048], P(('tp', 'ctx')), may hold values from 0.5 to 1.5
- block_order: int32 [2, 8], replicated, may hold values from 0 to 7, each once within a row
- cotangent: bfloat16 [2, 1024, 2048], P(None, 'ctx', 'tp'), may hold values from -6 to 6
Outputs:
- output: float32 [2, 1024, 2048], P(None, 'ctx', 'tp')
- grad_input: float32 [2, 1024, 2048], P(None, 'ctx', 'tp')
- grad_query: float32 [2048, 2048], P('ctx', 'tp')
- grad_key: float32 [2048, 2048], P('ctx', 'tp')
- grad_value: float32 [2048, 2048], P('ctx', 'tp')
- grad_output_proj: float32 [2048, 2048], P('tp', 'ctx')
- grad_gate: float32 [2048, 8192], P('ctx', 'tp')
- grad_up: float32 [2048, 8192], P('ctx', 'tp')
- grad_down: float32 [8192, 2048], P('tp', 'ctx')
- grad_gain_query: float32 [2048], P(('tp', 'ctx'))
- grad_gain_key: float32 [2048], P(('tp', 'ctx'))
- grad_gain_attention: float32 [2048], P(('tp', 'ctx'))
- grad_gain_feedforward: float32 [2048], P(('tp', 'ctx'))
Inputs may be any that keep to these rules, and one draw needn't show every extreme that they name: Each row of block_order names each of the 8 blocks of a sequence once.
All inputs are finite; a program needn't handle non-finite values.
Results may differ from a plain program's by a relative error of at most 0.023.
Values may be sent and summed in bfloat16 or wider, within the bound.
A program may use at most 192 MiB of HBM per device.

v0:
```python
import jax
import jax.numpy as jnp
from jax import lax
from jax.sharding import PartitionSpec as P

HD = 128


EPS = 1e-06
THETA = 500000.0
NEGATIVE = -1e30


def full_width(value):
    return lax.all_gather(value, "tp", axis=2, tiled=True)


def share(value):
    return lax.psum_scatter(value, "tp", scatter_dimension=2, tiled=True)


def tp_total(values):
    return lax.psum(values, "tp")


def rotary_tables(positions):
    half_dim = HD // 2
    frequency = THETA ** (-2.0 * jnp.arange(half_dim, dtype=jnp.float32) / HD)
    angles = positions.astype(jnp.float32)[..., None] * frequency
    return (jnp.cos(angles)[..., None, :], jnp.sin(angles)[..., None, :])


def rotate(value, cosine, sine):
    half_dim = value.shape[-1] // 2
    first, second = (value[..., :half_dim], value[..., half_dim:])
    return jnp.concatenate(
        [first * cosine - second * sine, second * cosine + first * sine], axis=-1
    )


def unrotate(grad, cosine, sine):
    half_dim = grad.shape[-1] // 2
    first, second = (grad[..., :half_dim], grad[..., half_dim:])
    return jnp.concatenate(
        [first * cosine + second * sine, second * cosine - first * sine], axis=-1
    )


def key_positions(block_order, start, count, block_len):
    slots = start + jnp.arange(count, dtype=jnp.int32)
    owner = slots // block_len
    ranks = jnp.arange(block_order.shape[1], dtype=jnp.int32)
    chosen = jnp.sum(
        jnp.where(owner[None, :, None] == ranks[None, None, :], block_order[:, None, :], 0), axis=2
    )
    return chosen * block_len + slots % block_len


def span_of():
    return 512


def shards(
    tokens,
    w_query,
    w_key,
    w_value,
    w_output,
    w_gate,
    w_up,
    w_down,
    gain_query,
    gain_key,
    gain_attention,
    gain_feedforward,
    block_order,
    cotangent,
):
    gathered = (
        lax.all_gather(w_query, "ctx", axis=0, tiled=True),
        lax.all_gather(w_key, "ctx", axis=0, tiled=True),
        lax.all_gather(w_value, "ctx", axis=0, tiled=True),
        lax.all_gather(w_output, "ctx", axis=1, tiled=True),
        lax.all_gather(w_gate, "ctx", axis=0, tiled=True),
        lax.all_gather(w_up, "ctx", axis=0, tiled=True),
        lax.all_gather(w_down, "ctx", axis=1, tiled=True),
        lax.all_gather(gain_query, "ctx", axis=0, tiled=True),
        lax.all_gather(gain_key, "ctx", axis=0, tiled=True),
        lax.all_gather(gain_attention, "ctx", axis=0, tiled=True),
        lax.all_gather(gain_feedforward, "ctx", axis=0, tiled=True),
    )
    wq_full, wk_full, wv_full, wo_full, wg_full, wu_full, wd_full = gathered[:7]
    g_query = gathered[7].astype(jnp.float32)
    g_key = gathered[8].astype(jnp.float32)
    g_attn = gathered[9].astype(jnp.float32)
    g_feed = gathered[10].astype(jnp.float32)
    seq_count, block_len, local_width = tokens.shape
    row_count = seq_count * block_len
    scale = HD ** (-0.5)
    tok_full = full_width(tokens)
    tok_rows = tok_full.reshape(row_count, -1)
    width = tok_rows.shape[1]
    queries = jnp.dot(tok_rows, wq_full, preferred_element_type=jnp.float32)
    keys_raw = jnp.dot(tok_rows, wk_full, preferred_element_type=jnp.float32)
    values_raw = jnp.dot(tok_rows, wv_full, preferred_element_type=jnp.float32)
    head_width = queries.shape[1]
    head_count = head_width // HD
    q_squares, k_squares = tp_total(
        (jnp.sum(queries * queries, axis=1), jnp.sum(keys_raw * keys_raw, axis=1))
    )
    q_inverse = lax.rsqrt(q_squares / width + EPS)[:, None]
    k_inverse = lax.rsqrt(k_squares / width + EPS)[:, None]
    q_normed = queries * q_inverse * g_query
    k_normed = keys_raw * k_inverse * g_key
    ctx_rank = lax.axis_index("ctx")
    ranks = jnp.arange(block_order.shape[1], dtype=jnp.int32)
    my_block = jnp.sum(jnp.where(ranks[None, :] == ctx_rank, block_order, 0), axis=1)
    q_pos = my_block[:, None] * block_len + jnp.arange(block_len, dtype=jnp.int32)[None, :]
    cosine, sine = rotary_tables(q_pos)
    q_rot = rotate(q_normed.reshape(seq_count, block_len, head_count, HD), cosine, sine).astype(
        jnp.bfloat16
    )
    k_rot = rotate(k_normed.reshape(seq_count, block_len, head_count, HD), cosine, sine).astype(
        jnp.bfloat16
    )
    k_flat = k_rot.reshape(seq_count, block_len, head_width)
    v_flat = values_raw.astype(jnp.bfloat16).reshape(seq_count, block_len, head_width)

    def stat_block(state, key_piece, k_pos):
        run_max, run_sum = state
        scores = (
            jnp.einsum("sqhd,skhd->shqk", q_rot, key_piece, preferred_element_type=jnp.float32)
            * scale
        )
        visible = k_pos[:, None, None, :] <= q_pos[:, None, :, None]
        scores = jnp.where(visible, scores, NEGATIVE)
        new_max = jnp.maximum(run_max, jnp.max(scores, axis=-1))
        weights = jnp.where(visible, jnp.exp(scores - new_max[..., None]), 0.0)
        run_sum = run_sum * jnp.exp(run_max - new_max) + jnp.sum(weights, axis=-1)
        return (new_max, run_sum)

    init = (
        jnp.full((seq_count, head_count, block_len), NEGATIVE, jnp.float32),
        jnp.zeros((seq_count, head_count, block_len), jnp.float32),
    )
    fold_key_all = lax.all_gather(k_flat, "ctx", axis=1, tiled=True)
    count = fold_key_all.shape[1]
    span = span_of()

    def fold_one_span(step_index, inner):
        offset = step_index * span
        key_piece = lax.dynamic_slice_in_dim(fold_key_all, offset, span, 1).reshape(
            seq_count, span, head_count, HD
        )
        k_pos = key_positions(block_order, offset, span, block_len)
        return stat_block(inner, key_piece, k_pos)

    run_max, run_sum = lax.fori_loop(0, count // span, fold_one_span, init)
    key_all, val_all = (
        lax.all_gather(k_flat, "ctx", axis=1, tiled=True),
        lax.all_gather(v_flat, "ctx", axis=1, tiled=True),
    )
    log_total = run_max + jnp.log(run_sum)
    total_len = key_all.shape[1]
    total_span = span_of()

    def value_span(step_index, acc):
        offset = step_index * total_span
        key_piece = lax.dynamic_slice_in_dim(key_all, offset, total_span, 1).reshape(
            seq_count, total_span, head_count, HD
        )
        val_piece = lax.dynamic_slice_in_dim(val_all, offset, total_span, 1).reshape(
            seq_count, total_span, head_count, HD
        )
        k_pos = key_positions(block_order, offset, total_span, block_len)
        scores = (
            jnp.einsum("sqhd,skhd->shqk", q_rot, key_piece, preferred_element_type=jnp.float32)
            * scale
        )
        visible = k_pos[:, None, None, :] <= q_pos[:, None, :, None]
        weights = jnp.where(visible, jnp.exp(scores - log_total[..., None]), 0.0).astype(
            jnp.bfloat16
        )
        return acc + jnp.einsum(
            "shqk,skhd->sqhd", weights, val_piece, preferred_element_type=jnp.float32
        )

    attended = lax.fori_loop(
        0,
        total_len // total_span,
        value_span,
        jnp.zeros((seq_count, block_len, head_count, HD), jnp.float32),
    )
    attn_bf = attended.reshape(row_count, head_width).astype(jnp.bfloat16)
    attn_proj = share(
        jnp.dot(attn_bf, wo_full, preferred_element_type=jnp.float32).reshape(
            seq_count, block_len, -1
        )
    )
    (a_squares,) = tp_total((jnp.sum(attn_proj * attn_proj, axis=2),))
    a_inverse = lax.rsqrt(a_squares / width + EPS)[..., None]
    hidden_state = tokens.astype(jnp.float32) + attn_proj * a_inverse * g_attn
    hidden_rows = full_width(hidden_state.astype(jnp.bfloat16)).reshape(row_count, -1)
    gate = jnp.dot(hidden_rows, wg_full, preferred_element_type=jnp.float32)
    up_vals = jnp.dot(hidden_rows, wu_full, preferred_element_type=jnp.float32)
    sigma = jax.nn.sigmoid(gate)
    activation = (gate * sigma * up_vals).astype(jnp.bfloat16)
    mixed = share(
        jnp.dot(activation, wd_full, preferred_element_type=jnp.float32).reshape(
            seq_count, block_len, -1
        )
    )
    (m_squares,) = tp_total((jnp.sum(mixed * mixed, axis=2),))
    m_inverse = lax.rsqrt(m_squares / width + EPS)[..., None]
    output = hidden_state + mixed * m_inverse * g_feed
    upstream = cotangent.astype(jnp.float32)
    (m_dots,) = tp_total((jnp.sum(g_feed * upstream * mixed, axis=2),))
    d_mixed = m_inverse * (g_feed * upstream) - mixed * m_inverse**3 * (m_dots / width)[..., None]
    d_gfeed = jnp.sum(upstream * mixed * m_inverse, axis=(0, 1))
    d_mixed_rows = full_width(d_mixed.astype(jnp.bfloat16)).reshape(row_count, -1)
    grad_down = jnp.dot(activation.T, d_mixed_rows, preferred_element_type=jnp.float32)
    d_act = jnp.dot(d_mixed_rows, wd_full.T, preferred_element_type=jnp.float32)
    d_up_bf = (d_act * gate * sigma).astype(jnp.bfloat16)
    d_gate_bf = (d_act * up_vals * sigma * (1.0 + gate * (1.0 - sigma))).astype(jnp.bfloat16)
    grad_gate = jnp.dot(hidden_rows.T, d_gate_bf, preferred_element_type=jnp.float32)
    grad_up = jnp.dot(hidden_rows.T, d_up_bf, preferred_element_type=jnp.float32)
    back_ff = jnp.dot(d_gate_bf, wg_full.T, preferred_element_type=jnp.float32) + jnp.dot(
        d_up_bf, wu_full.T, preferred_element_type=jnp.float32
    )
    d_hidden = upstream + share(back_ff.reshape(seq_count, block_len, -1))
    (a_dots,) = tp_total((jnp.sum(g_attn * d_hidden * attn_proj, axis=2),))
    d_attn = (
        a_inverse * (g_attn * d_hidden) - attn_proj * a_inverse**3 * (a_dots / width)[..., None]
    )
    d_gattn = jnp.sum(d_hidden * attn_proj * a_inverse, axis=(0, 1))
    d_attn_rows = full_width(d_attn.astype(jnp.bfloat16)).reshape(row_count, -1)
    grad_outproj = jnp.dot(attn_bf.T, d_attn_rows, preferred_element_type=jnp.float32)
    d_heads = jnp.dot(d_attn_rows, wo_full.T, preferred_element_type=jnp.float32).reshape(
        seq_count, block_len, head_count, HD
    )
    deltas = jnp.sum(d_heads * attended, axis=3).transpose(0, 2, 1)
    d_heads_bf = d_heads.astype(jnp.bfloat16)

    def grad_block(key_piece, val_piece, k_pos):
        scores = (
            jnp.einsum("sqhd,skhd->shqk", q_rot, key_piece, preferred_element_type=jnp.float32)
            * scale
        )
        visible = k_pos[:, None, None, :] <= q_pos[:, None, :, None]
        probs = jnp.where(visible, jnp.exp(scores - log_total[..., None]), 0.0)
        d_probs = jnp.einsum(
            "sqhd,skhd->shqk", d_heads_bf, val_piece, preferred_element_type=jnp.float32
        )
        d_scores = (probs * (d_probs - deltas[..., None])).astype(jnp.bfloat16)
        return (probs, d_scores)

    def query_span(step_index, acc):
        offset = step_index * total_span
        key_piece = lax.dynamic_slice_in_dim(key_all, offset, total_span, 1).reshape(
            seq_count, total_span, head_count, HD
        )
        val_piece = lax.dynamic_slice_in_dim(val_all, offset, total_span, 1).reshape(
            seq_count, total_span, head_count, HD
        )
        k_pos = key_positions(block_order, offset, total_span, block_len)
        probs, d_scores = grad_block(key_piece, val_piece, k_pos)
        return (
            acc
            + jnp.einsum("shqk,skhd->sqhd", d_scores, key_piece, preferred_element_type=jnp.float32)
            * scale
        )

    d_qrot = lax.fori_loop(
        0,
        total_len // total_span,
        query_span,
        jnp.zeros((seq_count, block_len, head_count, HD), jnp.float32),
    )
    count = block_len * lax.axis_size("ctx")
    key_span = span_of()

    def key_one_span(step_index, buffer):
        offset = step_index * key_span
        key_piece = lax.dynamic_slice_in_dim(key_all, offset, key_span, 1).reshape(
            seq_count, key_span, head_count, HD
        )
        val_piece = lax.dynamic_slice_in_dim(val_all, offset, key_span, 1).reshape(
            seq_count, key_span, head_count, HD
        )
        k_pos = key_positions(block_order, offset, key_span, block_len)
        probs, d_scores = grad_block(key_piece, val_piece, k_pos)
        d_keyp = (
            jnp.einsum("shqk,sqhd->skhd", d_scores, q_rot, preferred_element_type=jnp.float32)
            * scale
        )
        d_valp = jnp.einsum(
            "shqk,sqhd->skhd",
            probs.astype(jnp.bfloat16),
            d_heads_bf,
            preferred_element_type=jnp.float32,
        )
        both = jnp.concatenate(
            [
                d_keyp.reshape(seq_count, key_span, head_width),
                d_valp.reshape(seq_count, key_span, head_width),
            ],
            axis=2,
        )
        return lax.dynamic_update_slice_in_dim(buffer, both.transpose(1, 0, 2), offset, 0)

    key_sums = (
        lax.psum_scatter(
            lax.fori_loop(
                0,
                count // key_span,
                key_one_span,
                jnp.zeros((count, seq_count, 2 * head_width), jnp.float32),
            ).astype(jnp.bfloat16),
            "ctx",
            scatter_dimension=0,
            tiled=True,
        )
        .astype(jnp.float32)
        .transpose(1, 0, 2)
    )
    d_krot = key_sums[..., :head_width].reshape(seq_count, block_len, head_count, HD)
    d_values = key_sums[..., head_width:].reshape(row_count, head_width)
    dq_normed = unrotate(d_qrot, cosine, sine).reshape(row_count, head_width)
    dk_normed = unrotate(d_krot, cosine, sine).reshape(row_count, head_width)
    q_dots, k_dots = tp_total(
        (
            jnp.sum(g_query * dq_normed * queries, axis=1),
            jnp.sum(g_key * dk_normed * keys_raw, axis=1),
        )
    )
    d_queries = (
        q_inverse * (g_query * dq_normed) - queries * q_inverse**3 * (q_dots / width)[:, None]
    )
    d_keys = k_inverse * (g_key * dk_normed) - keys_raw * k_inverse**3 * (k_dots / width)[:, None]
    d_gquery = jnp.sum(dq_normed * queries * q_inverse, axis=0)
    d_gkey = jnp.sum(dk_normed * keys_raw * k_inverse, axis=0)
    dq_bf = d_queries.astype(jnp.bfloat16)
    dk_bf = d_keys.astype(jnp.bfloat16)
    dv_bf = d_values.astype(jnp.bfloat16)
    grad_q = jnp.dot(tok_rows.T, dq_bf, preferred_element_type=jnp.float32)
    grad_k = jnp.dot(tok_rows.T, dk_bf, preferred_element_type=jnp.float32)
    grad_v = jnp.dot(tok_rows.T, dv_bf, preferred_element_type=jnp.float32)
    back_attn = (
        jnp.dot(dq_bf, wq_full.T, preferred_element_type=jnp.float32)
        + jnp.dot(dk_bf, wk_full.T, preferred_element_type=jnp.float32)
        + jnp.dot(dv_bf, wv_full.T, preferred_element_type=jnp.float32)
    )
    grad_input = d_hidden + share(back_attn.reshape(seq_count, block_len, -1))
    summed = (
        lax.psum_scatter(
            grad_q.astype(jnp.bfloat16), "ctx", scatter_dimension=0, tiled=True
        ).astype(jnp.float32),
        lax.psum_scatter(
            grad_k.astype(jnp.bfloat16), "ctx", scatter_dimension=0, tiled=True
        ).astype(jnp.float32),
        lax.psum_scatter(
            grad_v.astype(jnp.bfloat16), "ctx", scatter_dimension=0, tiled=True
        ).astype(jnp.float32),
        lax.psum_scatter(
            grad_outproj.astype(jnp.bfloat16), "ctx", scatter_dimension=1, tiled=True
        ).astype(jnp.float32),
        lax.psum_scatter(
            grad_gate.astype(jnp.bfloat16), "ctx", scatter_dimension=0, tiled=True
        ).astype(jnp.float32),
        lax.psum_scatter(
            grad_up.astype(jnp.bfloat16), "ctx", scatter_dimension=0, tiled=True
        ).astype(jnp.float32),
        lax.psum_scatter(
            grad_down.astype(jnp.bfloat16), "ctx", scatter_dimension=1, tiled=True
        ).astype(jnp.float32),
        lax.psum_scatter(
            d_gquery.astype(jnp.bfloat16), "ctx", scatter_dimension=0, tiled=True
        ).astype(jnp.float32),
        lax.psum_scatter(
            d_gkey.astype(jnp.bfloat16), "ctx", scatter_dimension=0, tiled=True
        ).astype(jnp.float32),
        lax.psum_scatter(
            d_gattn.astype(jnp.bfloat16), "ctx", scatter_dimension=0, tiled=True
        ).astype(jnp.float32),
        lax.psum_scatter(
            d_gfeed.astype(jnp.bfloat16), "ctx", scatter_dimension=0, tiled=True
        ).astype(jnp.float32),
    )
    return (
        output,
        grad_input,
        summed[0],
        summed[1],
        summed[2],
        summed[3],
        summed[4],
        summed[5],
        summed[6],
        summed[7],
        summed[8],
        summed[9],
        summed[10],
    )


def solution(mesh):
    placed = (
        P(None, "ctx", "tp"),
        P("ctx", "tp"),
        P("ctx", "tp"),
        P("ctx", "tp"),
        P("tp", "ctx"),
        P("ctx", "tp"),
        P("ctx", "tp"),
        P("tp", "ctx"),
        P(("tp", "ctx")),
        P(("tp", "ctx")),
        P(("tp", "ctx")),
        P(("tp", "ctx")),
        P(),
        P(None, "ctx", "tp"),
    )
    return jax.shard_map(
        shards,
        mesh=mesh,
        in_specs=placed,
        out_specs=(
            P(None, "ctx", "tp"),
            P(None, "ctx", "tp"),
            P("ctx", "tp"),
            P("ctx", "tp"),
            P("ctx", "tp"),
            P("tp", "ctx"),
            P("ctx", "tp"),
            P("ctx", "tp"),
            P("tp", "ctx"),
            P(("tp", "ctx")),
            P(("tp", "ctx")),
            P(("tp", "ctx")),
            P(("tp", "ctx")),
        ),
        check_vma=False,
    )
```

profile of v0, /device:TPU:0, one launch (start us, length us, event | category | flops | bytes accessed | tf_op | source)
XLA Modules:
  0.0 1228.2 jit_solution(2527298165793283409)
XLA Ops:
  15.4 16.1 %all-reduce.11 = (bf16[512]{0:T(512)(128)(2,1)S(1)}, bf16[512]{0:T(512)(128)(2,1)S(1)}, bf16[512]{0:T(512)(128)(2,1)}, bf16[512]{0:T(512)(128)(2,1)S(1)}) all-reduce(bf16[512]{0:T(512)(128)(2,1)S(1)} %dynamic-update-slice, bf16[512]{0:T(512)(128)(2,1)S(1)} %dynamic-update-slice.1, ...), channel_id=1, replica_groups=mesh['ctx'=8,'tp'=4] {'ctx'}, use_global_device_ids=true, to_apply=%add | all-reduce | flops 2048 | bytes 8192
  33.9 6.3 all-gather.14.cloned.1.call-done
  40.3 29.1 %all-gather.20.cloned.1.call-done = bf16[2048,512]{1,0:T(8,128)(2,1)} async-done(((bf16[256,512]{1,0:T(8,128)(2,1)}), bf16[2048,512]{1,0:T(8,128)(2,1)}) %all-gather.20.cloned.1.call-update) | async-done | bytes 2097168 | tf_op jit(solution)/shard_map/all_gather | solution.py:81
  72.1 27.0 %all-gather.24.cloned.1.call-done = bf16[2048,512]{1,0:T(8,128)(2,1)} async-done(((bf16[256,512]{1,0:T(8,128)(2,1)}), bf16[2048,512]{1,0:T(8,128)(2,1)}) %all-gather.24.cloned.1.call-update) | async-done | bytes 2097168 | tf_op jit(solution)/shard_map/all_gather | solution.py:80
  101.5 11.7 all-reduce.9
  116.8 11.8 all-gather.16.cloned.1.call-done
  132.8 26.2 %all-gather.22.cloned.1.call-done = bf16[2,1024,512]{1,2,0:T(8,128)(2,1)} async-done(((bf16[2,128,512]{1,2,0:T(8,128)(2,1)}), bf16[2,1024,512]{1,2,0:T(8,128)(2,1)}) %all-gather.22.cloned.1.call-update) | async-done | bytes 2097168 | tf_op jit(solution)/shard_map/all_gather | solution.py:160
  159.1 7.2 while.67
  166.2 23.3 %all-gather.18.cloned.1.call-done = bf16[2,1024,512]{1,2,0:T(8,128)(2,1)} async-done(((bf16[2,128,512]{1,2,0:T(8,128)(2,1)}), bf16[2,1024,512]{1,2,0:T(8,128)(2,1)}) %all-gather.18.cloned.1.call-update) | async-done | bytes 2097168 | tf_op jit(solution)/shard_map/all_gather | solution.py:161
  189.5 7.6 while.68
  197.2 22.3 %all-gather.26.cloned.1.call-done = bf16[512,2048]{1,0:T(8,128)(2,1)} async-done(((bf16[512,256]{1,0:T(8,128)(2,1)}), bf16[512,2048]{1,0:T(8,128)(2,1)}) %all-gather.26.cloned.1.call-update) | async-done | bytes 2097168 | tf_op jit(solution)/shard_map/all_gather | solution.py:83
  223.8 43.1 %reduce-scatter.15.cloned.1.call-done = f32[2,128,512]{2,1,0:T(8,128)} async-done(((f32[2,128,2048]{2,1,0:T(8,128)}), f32[2,128,512]{2,1,0:T(8,128)}) %reduce-scatter.15.cloned.1.call-update) | async-done | bytes 524304 | tf_op jit(solution)/shard_map/reduce_scatter | solution.py:19
  268.1 10.2 psum.58
  282.4 23.9 %all-gather.28.cloned.1.call-done = bf16[2,128,2048]{2,1,0:T(8,128)(2,1)} async-done(((bf16[2,128,512]{2,1,0:T(8,128)(2,1)}), bf16[2,128,2048]{2,1,0:T(8,128)(2,1)}) %all-gather.28.cloned.1.call-update) | async-done | bytes 1048592 | tf_op jit(solution)/shard_map/all_gather | solution.py:15
  306.2 55.4 %all-gather.30.cloned.1.call-done = bf16[2048,2048]{1,0:T(8,128)(2,1)} async-done(((bf16[256,2048]{1,0:T(8,128)(2,1)}), bf16[2048,2048]{1,0:T(8,128)(2,1)}) %all-gather.30.cloned.1.call-update) | async-done | bytes 8388624 | tf_op jit(solution)/shard_map/all_gather | solution.py:84
  361.6 7.4 fusion.76
  369.1 48.7 %all-gather.32.cloned.1.call-done = bf16[2048,2048]{1,0:T(8,128)(2,1)} async-done(((bf16[256,2048]{1,0:T(8,128)(2,1)}), bf16[2048,2048]{1,0:T(8,128)(2,1)}) %all-gather.32.cloned.1.call-update) | async-done | bytes 8388624 | tf_op jit(solution)/shard_map/all_gather | solution.py:85
  417.8 7.8 multiply_convert_fusion.2
  425.6 49.8 %all-gather.34.cloned.1.call-done = bf16[2048,2048]{1,0:T(8,128)(2,1)} async-done(((bf16[2048,256]{1,0:T(8,128)(2,1)}), bf16[2048,2048]{1,0:T(8,128)(2,1)}) %all-gather.34.cloned.1.call-update) | async-done | bytes 8388624 | tf_op jit(solution)/shard_map/all_gather | solution.py:86
  475.4 7.0 fusion.77
  482.6 43.7 %reduce-scatter.17.cloned.1.call-done = f32[2,128,512]{2,1,0:T(8,128)} async-done(((f32[2,128,2048]{2,1,0:T(8,128)}), f32[2,128,512]{2,1,0:T(8,128)}) %reduce-scatter.17.cloned.1.call-update) | async-done | bytes 524304 | tf_op jit(solution)/shard_map/reduce_scatter | solution.py:19
  527.5 10.2 psum.59
  538.9 8.6 psum.60
  549.9 26.8 %all-gather.36.cloned.1.call-done = bf16[2,128,2048]{2,1,0:T(8,128)(2,1)} async-done(((bf16[2,128,512]{2,1,0:T(8,128)(2,1)}), bf16[2,128,2048]{2,1,0:T(8,128)(2,1)}) %all-gather.36.cloned.1.call-update) | async-done | bytes 1048592 | tf_op jit(solution)/shard_map/all_gather | solution.py:15
  576.7 7.8 multiply_convert_fusion
  584.5 6.5 fusion.78
  591.1 7.1 convolution_add_fusion.2
  598.2 43.1 %reduce-scatter.19.cloned.1.call-done = f32[2,128,512]{2,1,0:T(8,128)} async-done(((f32[2,128,2048]{2,1,0:T(8,128)}), f32[2,128,512]{2,1,0:T(8,128)}) %reduce-scatter.19.cloned.1.call-update) | async-done | bytes 524304 | tf_op jit(solution)/shard_map/reduce_scatter | solution.py:19
  643.0 10.1 psum.61
  655.5 26.0 %all-gather.38.cloned.1.call-done = bf16[2,128,2048]{2,1,0:T(8,128)(2,1)} async-done(((bf16[2,128,512]{2,1,0:T(8,128)(2,1)}), bf16[2,128,2048]{2,1,0:T(8,128)(2,1)}) %all-gather.38.cloned.1.call-update) | async-done | bytes 1048592 | tf_op jit(solution)/shard_map/all_gather | solution.py:15
  687.4 26.2 %while.66 = (s32[]{:T(128)}, bf16[1024,2,1024]{0,2,1:T(8,128)(2,1)}, s32[2,8]{1,0:T(2,128)S(1)}, bf16[2,1024,512]{1,2,0:T(8,128)(2,1)S(1)}, bf16[2,128,4,128]{1,...) while((s32[]{:T(128)}, ...), condition=%wide.region_32.33_spmd.clone, body=%wide.region_30.32_spmd.clone.sunk | while | flops 545946880 | bytes 23374116 | solution.py:313
  713.6 6.5 copy.184
  725.5 7.2 convolution_convert_fusion
  734.0 6.9 convolution_convert_fusion.2
  740.9 7.1 convolution_convert_fusion.1
  749.8 18.8 %while.69 = (s32[]{:T(128)}, f32[2,128,4,128]{1,3,2,0:T(8,128)}, bf16[2,1024,512]{1,2,0:T(8,128)(2,1)S(1)}, s32[2,8]{1,0:T(2,128)S(1)}, bf16[2,128,4,128]{3,1,2,...) while((s32[]{:T(128)}, f32[2,128,4,128]{1,3,2,0:T(8,128)}, ...), condition=%wide.region_27.28_spmd.clone, body=%wide.region_25.27_spmd.clone.sunk | while | flops 406355200 | bytes 13412621 | solution.py:273
  755.1 4.1 fusion.181
  764.5 4.1 fusion.181
  779.1 11.9 all-reduce.8
  808.3 7.4 reduce-scatter.29.cloned.1.call-done
  817.5 12.5 %all-reduce.10 = (bf16[512]{0:T(512)(128)(2,1)S(1)}, bf16[512]{0:T(512)(128)(2,1)S(1)}, bf16[512]{0:T(512)(128)(2,1)S(1)}, bf16[512]{0:T(512)(128)(2,1)S(1)}) all-reduce(bf16[512]{0:T(512)(128)(2,1)S(1)} %get-tuple-element.1219, bf16[512]{0:T(512)(128)(2,1)S(1)} %get-tuple-element.1217, ...), channel_id=14, replica_groups=mesh['ctx'=8,'tp'=4] {'ctx'}, use_global_device_ids=true, to_apply=%region_45.46.clone | all-reduce | flops 2048 | bytes 8192
  832.3 58.2 %reduce-scatter.35.cloned.1.call-done = bf16[2048,256]{1,0:T(8,128)(2,1)} async-done(((bf16[2048,2048]{1,0:T(8,128)(2,1)}), bf16[2048,256]{1,0:T(8,128)(2,1)}) %reduce-scatter.35.cloned.1.call-update) | async-done | bytes 1048592 | tf_op jit(solution)/shard_map/reduce_scatter | solution.py:373
  893.2 72.2 %reduce-scatter.31.cloned.1.call-done = bf16[256,2048]{1,0:T(8,128)(2,1)} async-done(((bf16[2048,2048]{1,0:T(8,128)(2,1)}), bf16[256,2048]{1,0:T(8,128)(2,1)}) %reduce-scatter.31.cloned.1.call-update) | async-done | bytes 1048592 | tf_op jit(solution)/shard_map/reduce_scatter | solution.py:367
  968.2 72.2 %reduce-scatter.33.cloned.1.call-done = bf16[256,2048]{1,0:T(8,128)(2,1)} async-done(((bf16[2048,2048]{1,0:T(8,128)(2,1)}), bf16[256,2048]{1,0:T(8,128)(2,1)}) %reduce-scatter.33.cloned.1.call-update) | async-done | bytes 1048592 | tf_op jit(solution)/shard_map/reduce_scatter | solution.py:370
  1043.2 41.7 %reduce-scatter.25.cloned.1.call-done = bf16[256,512]{0,1:T(8,128)(2,1)} async-done(((bf16[2048,512]{0,1:T(8,128)(2,1)}), bf16[256,512]{0,1:T(8,128)(2,1)}) %reduce-scatter.25.cloned.1.call-update) | async-done | bytes 262160 | tf_op jit(solution)/shard_map/reduce_scatter | solution.py:358
  1086.7 42.6 %reduce-scatter.23.cloned.1.call-done = bf16[256,512]{0,1:T(8,128)(2,1)} async-done(((bf16[2048,512]{0,1:T(8,128)(2,1)}), bf16[256,512]{0,1:T(8,128)(2,1)}) %reduce-scatter.23.cloned.1.call-update) | async-done | bytes 262160 | tf_op jit(solution)/shard_map/reduce_scatter | solution.py:355
  1131.2 42.4 %reduce-scatter.27.cloned.1.call-done = bf16[256,512]{0,1:T(8,128)(2,1)} async-done(((bf16[2048,512]{0,1:T(8,128)(2,1)}), bf16[256,512]{0,1:T(8,128)(2,1)}) %reduce-scatter.27.cloned.1.call-update) | async-done | bytes 262160 | tf_op jit(solution)/shard_map/reduce_scatter | solution.py:361
  1175.5 44.1 %reduce-scatter.21.cloned.1.call-done = f32[2,128,512]{2,1,0:T(8,128)} async-done(((f32[2,128,2048]{2,1,0:T(8,128)}), f32[2,128,512]{2,1,0:T(8,128)}) %reduce-scatter.21.cloned.1.call-update) | async-done | bytes 524304 | tf_op jit(solution)/shard_map/reduce_scatter | solution.py:19
  (322 shorter events, 153.5 us)
Async XLA Ops:
  7.2 33.1 %all-gather.14.cloned.1.call-start = ((), (), s32[]{:S(2)}) async-start(), calls=%async_computation.12 | async-start | bytes 1310720 | tf_op jit(solution)/shard_map/all_gather | solution.py:15
  7.9 61.5 %all-gather.20.cloned.1.call-start = ((), (), s32[]{:S(2)}) async-start(), calls=%async_computation.15 | async-start | bytes 2359296 | tf_op jit(solution)/shard_map/all_gather | solution.py:81
  8.7 90.4 %all-gather.24.cloned.1.call-start = ((), (), s32[]{:S(2)}) async-start(), calls=%async_computation.17 | async-start | bytes 2359296 | tf_op jit(solution)/shard_map/all_gather | solution.py:80
  9.4 119.2 %all-gather.16.cloned.1.call-start = ((), (), s32[]{:S(2)}) async-start(), calls=%async_computation.13 | async-start | bytes 2359296 | tf_op jit(solution)/shard_map/all_gather | solution.py:82
  10.0 149.1 %all-gather.22.cloned.1.call-start = ((), (), s32[]{:S(2)}) async-start(), calls=%async_computation.16 | async-start | bytes 2359296 | tf_op jit(solution)/shard_map/all_gather | solution.py:160
  31.5 82.2 %copy-start.37 = (f32[512]{0:T(512)}, f32[512]{0:T(512)S(1)}, u32[]{:S(2)}) copy-start(f32[512]{0:T(512)S(1)} %convert_element_type.199) | copy-start | bytes 6148
  31.5 83.3 %copy-start.35 = (f32[512]{0:T(512)}, f32[512]{0:T(512)S(1)}, u32[]{:S(2)}) copy-start(f32[512]{0:T(512)S(1)} %convert_element_type.202) | copy-start | bytes 6148
  33.9 81.9 %copy-start.29 = (f32[2,128,64]{1,2,0:T(8,128)}, f32[2,128,64]{1,2,0:T(8,128)S(1)}, u32[]{:S(2)}) copy-start(f32[2,128,64]{1,2,0:T(8,128)S(1)} %get-tuple-element.1343) | copy-start | bytes 196612
  33.9 81.9 %copy-start.31 = (f32[2,128,64]{1,2,0:T(8,128)}, f32[2,128,64]{1,2,0:T(8,128)S(1)}, u32[]{:S(2)}) copy-start(f32[2,128,64]{1,2,0:T(8,128)S(1)} %get-tuple-element.1344) | copy-start | bytes 196612
  40.3 58.8 %copy-start.4 = (bf16[2,128,2048]{2,1,0:T(8,128)(2,1)S(1)}, bf16[2,128,2048]{2,1,0:T(8,128)(2,1)}, u32[]{:S(2)}) copy-start(bf16[2,128,2048]{2,1,0:T(8,128)(2,1)} %all-gather.14.cloned.1.call-done) | copy-start | bytes 3145732
  72.1 41.8 %copy-start.14 = (f32[256,512]{1,0:T(8,128)}, f32[256,512]{1,0:T(8,128)S(1)}, u32[]{:S(2)}) copy-start(f32[256,512]{1,0:T(8,128)S(1)} %get-tuple-element.1356) | copy-start | bytes 1572868
  101.4 13.4 %copy-start.12 = (f32[256,512]{1,0:T(8,128)}, f32[256,512]{1,0:T(8,128)S(1)}, u32[]{:S(2)}) copy-start(f32[256,512]{1,0:T(8,128)S(1)} %get-tuple-element.1358) | copy-start | bytes 1572868
  116.8 42.3 %copy-start.34 = (s32[2,8]{1,0:T(2,128)S(1)}, s32[2,8]{1,0:T(2,128)}, u32[]{:S(2)}) copy-start(s32[2,8]{1,0:T(2,128)} %param.34) | copy-start | bytes 196
  116.8 72.7 %all-gather.18.cloned.1.call-start = ((), (), s32[]{:S(2)}) async-start(), calls=%async_computation.14 | async-start | bytes 2359296 | tf_op jit(solution)/shard_map/all_gather | solution.py:161
  131.8 87.7 %all-gather.26.cloned.1.call-start = ((), (), s32[]{:S(2)}) async-start(), calls=%async_computation.18 | async-start | bytes 2359296 | tf_op jit(solution)/shard_map/all_gather | solution.py:83
  132.5 134.4 %reduce-scatter.15.cloned.1.call-start = ((), (), s32[]{:S(2)}) async-start(), calls=%async_computation.19 | async-start | bytes 2621440 | tf_op jit(solution)/shard_map/reduce_scatter | solution.py:19
  132.6 26.4 %copy-start.2 = (bf16[2,128,4,128]{1,3,2,0:T(8,128)(2,1)}, bf16[2,128,4,128]{1,3,2,0:T(8,128)(2,1)S(1)}, u32[]{:S(2)}) copy-start(bf16[2,128,4,128]{1,3,2,0:T(8,128)(2,1)S(1)} %pad_maximum_fusion.3) | copy-start | bytes 786436
  197.2 26.0 %copy-start.20 = (bf16[2,128,4,128]{1,3,2,0:T(8,128)(2,1)}, bf16[2,128,4,128]{1,3,2,0:T(8,128)(2,1)S(1)}, u32[]{:S(2)}) copy-start(bf16[2,128,4,128]{1,3,2,0:T(8,128)(2,1)S(1)} %convert_element_type.203) | copy-start | bytes 786436
  223.2 55.1 %copy-start.22 = (bf16[2,128,512]{2,1,0:T(8,128)(2,1)S(1)}, bf16[2,128,512]{2,1,0:T(8,128)(2,1)}, u32[]{:S(2)}) copy-start(bf16[2,128,512]{2,1,0:T(8,128)(2,1)} %param.22) | copy-start | bytes 786436
  223.2 83.1 %all-gather.28.cloned.1.call-start = ((), (), s32[]{:S(2)}) async-start(), calls=%async_computation.20 | async-start | bytes 1310720 | tf_op jit(solution)/shard_map/all_gather | solution.py:15
  280.2 81.4 %all-gather.30.cloned.1.call-start = ((), (), s32[]{:S(2)}) async-start(), calls=%async_computation.21 | async-start | bytes 9437184 | tf_op jit(solution)/shard_map/all_gather | solution.py:84
  280.8 137.0 %all-gather.32.cloned.1.call-start = ((), (), s32[]{:S(2)}) async-start(), calls=%async_computation.22 | async-start | bytes 9437184 | tf_op jit(solution)/shard_map/all_gather | solution.py:85
  281.5 193.9 %all-gather.34.cloned.1.call-start = ((), (), s32[]{:S(2)}) async-start(), calls=%async_computation.23 | async-start | bytes 9437184 | tf_op jit(solution)/shard_map/all_gather | solution.py:86
  282.1 244.2 %reduce-scatter.17.cloned.1.call-start = ((), (), s32[]{:S(2)}) async-start(), calls=%async_computation.24 | async-start | bytes 2621440 | tf_op jit(solution)/shard_map/reduce_scatter | solution.py:19
  361.6 56.2 %copy-start.8 = (bf16[2,128,2048]{2,1,0:T(8,128)(2,1)S(1)}, bf16[2,128,2048]{2,1,0:T(8,128)(2,1)}, u32[]{:S(2)}) copy-start(bf16[2,128,2048]{2,1,0:T(8,128)(2,1)} %all-gather.28.cloned.1.call-done) | copy-start | bytes 3145732
  425.6 56.8 %copy-start.25 = (bf16[256,2048]{1,0:T(8,128)(2,1)}, bf16[256,2048]{1,0:T(8,128)(2,1)S(1)}, u32[]{:S(2)}) copy-start(bf16[256,2048]{1,0:T(8,128)(2,1)S(1)} %get-tuple-element.1359) | copy-start | bytes 3145732
  482.5 55.1 %copy-start.10 = (bf16[2,128,512]{2,1,0:T(8,128)(2,1)S(1)}, bf16[2,128,512]{2,1,0:T(8,128)(2,1)}, u32[]{:S(2)}) copy-start(bf16[2,128,512]{2,1,0:T(8,128)(2,1)} %param.35) | copy-start | bytes 786436
  482.5 94.2 %all-gather.36.cloned.1.call-start = ((), (), s32[]{:S(2)}) async-start(), calls=%async_computation.25 | async-start | bytes 1310720 | tf_op jit(solution)/shard_map/all_gather | solution.py:15
  549.4 91.9 %reduce-scatter.19.cloned.1.call-start = ((), (), s32[]{:S(2)}) async-start(), calls=%async_computation.26 | async-start | bytes 2621440 | tf_op jit(solution)/shard_map/reduce_scatter | solution.py:19
  584.5 6.5 copy-start.28
  584.5 6.5 copy-start.27
  598.1 43.2 %copy-start.6 = (f32[2,128,512]{2,1,0:T(8,128)S(1)}, f32[2,128,512]{2,1,0:T(8,128)}, u32[]{:S(2)}) copy-start(f32[2,128,512]{2,1,0:T(8,128)} %reduce-scatter.15.cloned.1.call-done) | copy-start | bytes 1572868
  598.1 55.0 %copy-start.7 = (f32[2,128,512]{2,1,0:T(8,128)S(1)}, f32[2,128,512]{2,1,0:T(8,128)}, u32[]{:S(2)}) copy-start(f32[2,128,512]{2,1,0:T(8,128)} %reduce-scatter.17.cloned.1.call-done) | copy-start | bytes 1572868
  598.1 83.4 %all-gather.38.cloned.1.call-start = ((), (), s32[]{:S(2)}) async-start(), calls=%async_computation.27 | async-start | bytes 1310720 | tf_op jit(solution)/shard_map/all_gather | solution.py:15
  655.4 115.4 %reduce-scatter.37.cloned.1.call-start = ((), (), s32[]{:S(2)}) async-start(), calls=%async_computation.36 | async-start | bytes 4718592
  720.1 95.6 %reduce-scatter.29.cloned.1.call-start = ((), (), s32[]{:S(2)}) async-start(), calls=%async_computation.32 | async-start | bytes 2359296 | tf_op jit(solution)/shard_map/reduce_scatter | solution.py:364
  725.4 165.1 %reduce-scatter.35.cloned.1.call-start = ((), (), s32[]{:S(2)}) async-start(), calls=%async_computation.35 | async-start | bytes 9437184 | tf_op jit(solution)/shard_map/reduce_scatter | solution.py:373
  732.7 232.7 %reduce-scatter.31.cloned.1.call-start = ((), (), s32[]{:S(2)}) async-start(), calls=%async_computation.33 | async-start | bytes 9437184 | tf_op jit(solution)/shard_map/reduce_scatter | solution.py:367
  740.8 299.5 %reduce-scatter.33.cloned.1.call-start = ((), (), s32[]{:S(2)}) async-start(), calls=%async_computation.34 | async-start | bytes 9437184 | tf_op jit(solution)/shard_map/reduce_scatter | solution.py:370
  748.0 336.8 %reduce-scatter.25.cloned.1.call-start = ((), (), s32[]{:S(2)}) async-start(), calls=%async_computation.30 | async-start | bytes 2359296 | tf_op jit(solution)/shard_map/reduce_scatter | solution.py:358
  773.6 17.4 %copy-start.44 = (f32[256]{0:T(256)S(1)}, f32[256]{0:T(256)}, u32[]{:S(2)}) copy-start(f32[256]{0:T(256)} %get-tuple-element.1345) | copy-start | bytes 3076
  774.4 17.8 %copy-start.5 = (bf16[2,128,2048]{2,1,0:T(8,128)(2,1)S(1)}, bf16[2,128,2048]{2,1,0:T(8,128)(2,1)}, u32[]{:S(2)}) copy-start(bf16[2,128,2048]{2,1,0:T(8,128)(2,1)} %all-gather.14.cloned.1.call-done) | copy-start | bytes 3145732
  794.4 334.9 %reduce-scatter.23.cloned.1.call-start = ((), (), s32[]{:S(2)}) async-start(), calls=%async_computation.29 | async-start | bytes 2359296 | tf_op jit(solution)/shard_map/reduce_scatter | solution.py:355
  798.4 375.2 %reduce-scatter.27.cloned.1.call-start = ((), (), s32[]{:S(2)}) async-start(), calls=%async_computation.31 | async-start | bytes 2359296 | tf_op jit(solution)/shard_map/reduce_scatter | solution.py:361
  800.5 419.0 %reduce-scatter.21.cloned.1.call-start = ((), (), s32[]{:S(2)}) async-start(), calls=%async_computation.28 | async-start | bytes 2621440 | tf_op jit(solution)/shard_map/reduce_scatter | solution.py:19
  807.6 9.9 copy-start.45
  968.2 251.4 %copy-start.11 = (bf16[2,128,512]{2,1,0:T(8,128)(2,1)S(1)}, bf16[2,128,512]{2,1,0:T(8,128)(2,1)}, u32[]{:S(2)}) copy-start(bf16[2,128,512]{2,1,0:T(8,128)(2,1)} %param.35) | copy-start | bytes 786436
  968.2 251.4 %copy-start.17 = (f32[2,128,512]{2,1,0:T(8,128)S(1)}, f32[2,128,512]{2,1,0:T(8,128)}, u32[]{:S(2)}) copy-start(f32[2,128,512]{2,1,0:T(8,128)} %reduce-scatter.19.cloned.1.call-done) | copy-start | bytes 1572868
  (25 other events, 63.5 us)
Sparse Core Ops, SparseCore 0:
  9.6 30.6 all-gather.13
  42.2 27.1 all-gather.19
  71.3 27.7 all-gather.23
  100.8 27.7 all-gather.15
  130.9 28.0 all-gather.21
  161.4 28.0 all-gather.17
  191.4 28.0 all-gather.25
  223.3 43.6 reduce-scatter.14
  280.3 25.8 all-gather.27
  308.0 53.6 all-gather.29
  363.5 54.2 all-gather.31
  419.6 55.8 all-gather.33
  482.6 43.6 reduce-scatter.16
  549.5 27.0 all-gather.35
  598.3 42.9 reduce-scatter.18
  655.5 25.9 all-gather.37
  720.3 50.5 reduce-scatter.36
  774.6 41.1 reduce-scatter.28
  819.2 71.2 reduce-scatter.34
  893.8 71.5 reduce-scatter.30
  968.8 71.4 reduce-scatter.32
  1043.6 41.1 reduce-scatter.24
  1088.1 41.1 reduce-scatter.22
  1132.4 41.1 reduce-scatter.26
  1175.9 43.6 reduce-scatter.20
where the time goes:
time: 1240 us; the launch traced here: 1230 us
  waiting for transfers between devices  895 us (72%)
  matrix products  124 us (10%)
  blocking collectives  91.2 us (7%)
  local copies, waits for them, and re-layouts  52 us (4%)
  other arithmetic  47.4 us (4%)
  between operations  16.3 us (1%)
    reduce_scatter x4, waiting for transfers between devices, share(): return lax.psum_scatter(value, 'tp', scatter_dimension=2, tiled=True)  174 us
    all_gather x4, waiting for transfers between devices, full_width(): return lax.all_gather(value, 'tp', axis=2, tiled=True)  83.1 us
    reduce_scatter x1, waiting for transfers between devices, shards(): lax.psum_scatter(grad_up.astype(jnp.bfloat16), 'ctx', scatter_dimension=0...  72.2 us
    reduce_scatter x1, waiting for transfers between devices, shards(): lax.psum_scatter(grad_gate.astype(jnp.bfloat16), 'ctx', scatter_dimension...  72.2 us
    psum x6, blocking collectives, tp_total(): return lax.psum(values, 'tp')  62.6 us
    reduce_scatter x1, waiting for transfers between devices, shards(): lax.psum_scatter(grad_down.astype(jnp.bfloat16), 'ctx', scatter_dimension...  58.2 us
    all_gather x1, waiting for transfers between devices, shards(): lax.all_gather(w_gate, 'ctx', axis=0, tiled=True)  55.4 us
    all_gather x1, waiting for transfers between devices, shards(): lax.all_gather(w_down, 'ctx', axis=1, tiled=True)  49.8 us
  transfers between devices with their start and end apart: 25, of which 25 were waited for; matrix products, arithmetic and copies ran while one was open for 11% of the time, Pallas kernels for 0%

commit v1 on v0

--- a/solution.py
+++ b/solution.py
@@ -1,6 +1,10 @@
+import functools
+
 import jax
 import jax.numpy as jnp
 from jax import lax
+from jax.experimental import pallas as pl
+from jax.experimental.pallas import tpu as pltpu
 from jax.sharding import PartitionSpec as P
 
 HD = 128
@@ -403,6 +407,808 @@
     )
 
 
+MESH = pl.DeviceIdType.MESH
+NT = (((1,), (1,)), ((), ()))
+TN = (((0,), (0,)), ((), ()))
+F32 = jnp.float32
+BF16 = jnp.bfloat16
+COLS = (0, 1, 2, 4, 5)
+
+
+def layer_kernel(dims, *refs):
+    (chips, tps, seqs, blk, width, head_w, ff_w) = dims
+    rows = seqs * blk
+    both = 2 * rows
+    share_rows = rows // tps
+    feats = width // tps
+    heads = head_w // HD
+    slab = width // (2 * chips)
+    halves = (head_w, head_w, head_w, head_w, ff_w, ff_w, ff_w)
+    total = 2 * chips * blk
+    scale = HD ** (-0.5)
+    it = iter(refs)
+
+    def take(n):
+        return [next(it) for _ in range(n)]
+
+    (tok_in, cot_in) = take(2)
+    w_in = take(7)
+    (gtile, cosf, sinf, pos_row, pos_col) = take(5)
+    (out_ref, gin_ref, ggain_ref) = take(3)
+    rx_g = take(7)
+    w = take(7)
+    (tok, tok_t, hid, hid_t, dmix, dattn) = take(6)
+    (lin, fac, act, act_t, dgate, dup) = take(6)
+    (st_p, rx_p, st_z, rx_z, rx_f) = take(5)
+    (q_raw, k_raw, qkv, qa, probs, att_f, att_st, att, att_t) = take(9)
+    (dh, d_o, dk_acc, dv_acc, dqkv_st, dqkv) = take(6)
+    (sq_own, sq_rx, inv_q, inv_k) = take(4)
+    (cot, proj, hstate, mixed, dhid, stage) = take(6)
+    (gbuf, gall, gfull, gqk, gg_row, gg_rx1, gg_mid, gg_rx2) = take(8)
+    (ws, wr, gs, gr) = take(4)
+    (zs, zr, ps, pr) = take(4)
+    (rps, rpr, rzs, rzr) = take(4)
+    (ms, mr) = take(2)
+    (ss, sr) = take(2)
+    (as_, ar) = take(2)
+    (loc,) = take(1)
+
+    ctx = lax.axis_index("ctx")
+    z = lax.axis_index("tp")
+    c = ctx // 2
+    k = ctx % 2
+    ok = 1 - k
+    partner = c * 2 + ok
+
+    def zp(i):
+        return (z + i) % tps
+
+    def chip(i):
+        return (c + i) % chips
+
+    def ds(start, size):
+        return pl.ds(pl.multiple_of(start, size), size)
+
+    def remote(src, dst, ssem, rsem, to_ctx, to_z):
+        return pltpu.make_async_remote_copy(
+            src_ref=src,
+            dst_ref=dst,
+            send_sem=ssem,
+            recv_sem=rsem,
+            device_id=(to_ctx, to_z),
+            device_id_type=MESH,
+        )
+
+    peers = [(chip(i) * 2 + (k + d) % 2, z) for i in range(chips) for d in range(2) if i or d]
+    peers += [(ctx, zp(i)) for i in range(1, tps)]
+    peers += [(partner, zp(i)) for i in range(1, tps)]
+    barrier = pltpu.get_barrier_semaphore()
+    for peer in peers:
+        pl.semaphore_signal(barrier, inc=1, device_id=peer, device_id_type=MESH)
+
+    pending = []
+
+    def go(copy):
+        copy.start()
+        pending.append(copy)
+        return copy
+
+    def w_copy(m, i, d):
+        core = (k + d) % 2
+        half = halves[m]
+        if m in COLS:
+            src = w_in[m].at[:, ds(core * half, half)]
+            dst = w[m].at[ds(ctx * slab, slab), :]
+        else:
+            src = w_in[m].at[ds(core * half, half), :]
+            dst = w[m].at[:, ds(ctx * slab, slab)]
+        if i == 0 and d == 0:
+            return pltpu.make_async_copy(src, dst, loc.at[m])
+        return remote(src, dst, ws.at[m, 2 * i + d], wr.at[m, 2 * i + d], chip(i) * 2 + core, z)
+
+    slots = [(i, d) for i in range(chips) for d in range(2)]
+    w_live = {}
+
+    def send_w(m):
+        for i, d in slots:
+            copy = w_copy(m, i, d)
+            copy.start()
+            w_live[m, i, d] = copy
+            if i or d:
+                pending.append(copy)
+
+    def wait_w(m, i, d):
+        copy = w_live[m, i, d]
+        if i or d:
+            copy.wait_recv()
+        else:
+            copy.wait()
+
+    def send_g(m, chips_from=0, chips_to=chips):
+        half = halves[m]
+        for i in range(chips_from, chips_to):
+            for d in range(2):
+                to = chip(i) * 2 + (k + d) % 2
+                if m in COLS:
+                    src = w[m].at[ds(to * slab, slab), :]
+                    dst = rx_g[m].at[i, :, ds(k * half, half)]
+                else:
+                    src = w[m].at[:, ds(to * slab, slab)]
+                    dst = rx_g[m].at[i, ds(k * half, half), :]
+                if i or d:
+                    copy = remote(src, dst, gs.at[m, 2 * i + d], gr.at[m, 2 * i + d], to, z)
+                    go(copy)
+                    g_live.append(copy)
+                else:
+                    copy = pltpu.make_async_copy(src, dst, loc.at[8 + m])
+                    copy.start()
+                    g_own.append(copy)
+
+    g_live = []
+    g_own = []
+
+    own_tok = pltpu.make_async_copy(tok_in, tok.at[ds(k * rows, rows), ds(z * feats, feats)], loc.at[16])
+    own_tok.start()
+    own_cot = pltpu.make_async_copy(cot_in.at[ds(z * share_rows, share_rows), :], cot.at[:, ds(z * feats, feats)], loc.at[17])
+    own_cot.start()
+    own_gain = pltpu.make_async_copy(gtile, gbuf.at[ctx], loc.at[18])
+    own_gain.start()
+    pl.semaphore_wait(barrier, len(peers))
+
+    tok_z = []
+    for i in range(1, tps):
+        tok_z.append(go(remote(tok_in, tok.at[ds(k * rows, rows), ds(z * feats, feats)], zs.at[0, i - 1], zr.at[0, i - 1], ctx, zp(i))))
+    tok_p = [go(remote(tok_in, tok.at[ds(k * rows, rows), ds(z * feats, feats)], ps.at[0, 0], pr.at[0, 0], partner, z))]
+    gain1 = []
+    n = 0
+    for i, d in slots:
+        if i or d:
+            gain1.append(go(remote(gtile, gbuf.at[ctx], ms.at[0, n], mr.at[0, n], chip(i) * 2 + (k + d) % 2, z)))
+            n += 1
+    cot_z = []
+    for i in range(1, tps):
+        cot_z.append(go(remote(cot_in.at[ds(zp(i) * share_rows, share_rows), :], cot.at[:, ds(z * feats, feats)], ms.at[1, i - 1], mr.at[1, i - 1], ctx, zp(i))))
+    for m in (0, 1, 2, 3):
+        send_w(m)
+
+    own_gain.wait()
+    for copy in gain1:
+        copy.wait_recv()
+    own_gain2 = pltpu.make_async_copy(gbuf, gall.at[z], loc.at[19])
+    own_gain2.start()
+    gain2 = []
+    for i in range(1, tps):
+        gain2.append(go(remote(gbuf, gall.at[z], ms.at[2, i - 1], mr.at[2, i - 1], ctx, zp(i))))
+    for r in range(2):
+        pieces = [gbuf[4 * k + 2 * m, r : r + 1, :] + gbuf[4 * k + 2 * m + 1, r : r + 1, :] for m in range(head_w // 128)]
+        gqk[r : r + 1, :] = jnp.concatenate(pieces, axis=1)
+
+    own_tok.wait()
+    for i in range(1, tps):
+        tok_z[i - 1].wait_recv()
+        part = tok.at[ds(k * rows, rows), ds(((z - i) % tps) * feats, feats)]
+        tok_p.append(go(remote(part, part, ps.at[0, i], pr.at[0, i], partner, z)))
+    own_gain2.wait()
+    for copy in gain2:
+        copy.wait_recv()
+    for r in range(2):
+        pieces = []
+        for zz in range(tps):
+            for m in range(chips):
+                pieces.append(gall[zz, 2 * m, 2 + r : 3 + r, :] + gall[zz, 2 * m + 1, 2 + r : 3 + r, :])
+        gfull[r : r + 1, :] = jnp.concatenate(pieces, axis=1)
+    for copy in tok_p:
+        copy.wait_recv()
+
+    def row_of(value):
+        folded = value[:, :128]
+        for h in range(1, heads):
+            folded = folded + value[:, h * 128 : (h + 1) * 128]
+        return jnp.sum(jnp.transpose(folded), axis=0, keepdims=True)
+
+    def column_of(row):
+        return jnp.transpose(jnp.broadcast_to(row, (128, both)))
+
+    def totals(idx):
+        copies = []
+        n = 0
+        for i in range(tps):
+            for d in range(2):
+                if i or d:
+                    to = ctx if d == 0 else partner
+                    copies.append(go(remote(sq_own.at[idx], sq_rx.at[idx, n], ss.at[idx, n], sr.at[idx, n], to, zp(i))))
+                    n += 1
+        total = sq_own[idx]
+        for j, copy in enumerate(copies):
+            copy.wait_recv()
+            total = total + sq_rx[idx, j]
+        return total
+
+    for m in (0, 1, 2):
+        for i, d in slots:
+            wait_w(m, i, d)
+        value = jnp.dot(tok[...], w[m][...], preferred_element_type=F32)
+        if m == 0:
+            q_raw[...] = value
+            sq_own[0, 0:1, :] = row_of(value * value)
+        elif m == 1:
+            k_raw[...] = value
+            sq_own[0, 1:2, :] = row_of(value * value)
+            squares = None
+        else:
+            qkv[2] = value.astype(BF16).reshape(2, seqs, blk, head_w)
+    sq_own[0, 2:8, :] = jnp.zeros((6, both), F32)
+    squares = totals(0)
+    inverse = lax.rsqrt(squares / width + EPS)
+    inv_q[...] = column_of(inverse[0:1, :])
+    inv_k[...] = column_of(inverse[1:2, :])
+    for t, (raw, inv) in enumerate(((q_raw, inv_q), (k_raw, inv_k))):
+        for h in range(heads):
+            lanes = slice(h * HD, (h + 1) * HD)
+            normed = raw[:, lanes] * inv[...] * gqk[t : t + 1, lanes]
+            turned = normed * cosf[...] + pltpu.roll(normed, HD // 2, 1) * sinf[...]
+            qkv[t, :, :, :, lanes] = turned.astype(BF16).reshape(2, seqs, blk, HD)
+
+    def to_owner(idx, value, owned, stacked):
+        copies = []
+        for i in range(chips):
+            to = chip(i)
+            s, h = to // heads, to % heads
+            if stacked:
+                src = value.at[:, :, s, :, ds(h * HD, HD)]
+                dst = owned.at[:, ds(2 * c, 2)]
+            else:
+                src = value.at[:, s, :, ds(h * HD, HD)]
+                dst = owned.at[ds(2 * c, 2)]
+            if i:
+                copies.append(go(remote(src, dst, as_.at[idx, i - 1], ar.at[idx, i - 1], to * 2 + k, z)))
+            else:
+                own = pltpu.make_async_copy(src, dst, loc.at[20 + idx])
+                own.start()
+        return own, copies
+
+    def from_owner(idx, owned, value, stacked):
+        s, h = c // heads, c % heads
+        copies = []
+        for i in range(chips):
+            to = chip(i)
+            if stacked:
+                src = owned.at[:, ds(2 * to, 2)]
+                dst = value.at[:, :, s, :, ds(h * HD, HD)]
+            else:
+                src = owned.at[ds(2 * to, 2)]
+                dst = value.at[:, s, :, ds(h * HD, HD)]
+            if i:
+                copies.append(go(remote(src, dst, as_.at[idx, i - 1], ar.at[idx, i - 1], to * 2 + k, z)))
+            else:
+                own = pltpu.make_async_copy(src, dst, loc.at[20 + idx])
+                own.start()
+        return own, copies
+
+    def arrive(pair):
+        own, copies = pair
+        own.wait()
+        for copy in copies:
+            copy.wait_recv()
+
+    arrive(to_owner(0, qkv, qa, True))
+    step = 2 * blk
+
+    def attend(i, carry):
+        here = ds(i * step, step)
+        q = qa[0, pl.ds(2 * i, 2)].reshape(step, HD)
+        s = lax.dot_general(q, qa[1].reshape(total, HD), NT, preferred_element_type=F32) * scale
+        visible = pos_row[0:1, :] <= pos_col[here, 0:1]
+        s = jnp.where(visible, s, NEGATIVE)
+        top = jnp.max(s, axis=1, keepdims=True)
+        e = jnp.where(visible, jnp.exp(s - top), 0.0)
+        p = (e * (1.0 / jnp.sum(e, axis=1, keepdims=True))).astype(BF16)
+        probs[here, :] = p
+        o = jnp.dot(p, qa[2].reshape(total, HD), preferred_element_type=F32)
+        att_f[here, :] = o
+        att_st[pl.ds(2 * i, 2)] = o.astype(BF16).reshape(2, blk, HD)
+        return carry
+
+    lax.fori_loop(0, chips, attend, 0)
+    back = from_owner(1, att_st, att, False)
+    for m in (4, 5, 6):
+        send_w(m)
+    for s in range(width // 256):
+        tok_t[s * 256 : (s + 1) * 256, :] = jnp.transpose(tok[:, s * 256 : (s + 1) * 256])
+    arrive(back)
+    for i, d in slots:
+        wait_w(3, i, d)
+
+    cw = feats
+    rs_live = {}
+
+    def rp_copy(idx, i, off):
+        return remote(st_p.at[:, ds(off, cw)], rx_p.at[idx % 2, :, ds(off, cw)], rps.at[idx, i], rpr.at[idx, i], partner, z)
+
+    def rz_copy(idx, i, j, off):
+        return remote(
+            st_z.at[ds(zp(j) * share_rows, share_rows), ds(off, cw)],
+            rx_z.at[idx % 2, j - 1, :, ds(off, cw)],
+            rzs.at[idx, i, j - 1],
+            rzr.at[idx, i, j - 1],
+            ctx,
+            zp(j),
+        )
+
+    def reduce_rows(idx, partial, offset, before=None):
+        def one(i):
+            off = offset(i)
+            if before is not None:
+                before(i)
+            st_p[:, ds(off, cw)] = partial(ok, off).astype(BF16)
+            rp_copy(idx, i, off).start()
+            mine = partial(k, off)
+            rp_copy(idx, i, off).wait_recv()
+            st_z[:, ds(off, cw)] = (mine + rx_p[idx % 2, :, ds(off, cw)].astype(F32)).astype(BF16)
+            for j in range(1, tps):
+                rz_copy(idx, i, j, off).start()
+
+        def finish(i):
+            off = offset(i)
+            for j in range(1, tps):
+                rz_copy(idx, i, j, off).wait_recv()
+                rz_copy(idx, i, j, off).wait_send()
+            rp_copy(idx, i, off).wait_send()
+
+        if before is None:
+            lax.fori_loop(0, tps, lambda i, x: (one(i), x)[1], 0)
+        else:
+            for i in range(tps):
+                one(i)
+        lax.fori_loop(0, tps, lambda i, x: (finish(i), x)[1], 0)
+        mine = st_z[ds(z * share_rows, share_rows), :].astype(F32)
+        for j in range(tps - 1):
+            mine = mine + rx_z[idx % 2, j].astype(F32)
+        return mine
+
+    def straight(i):
+        return i * cw
+
+    def mean_of(value):
+        return jnp.sum(value, axis=1, keepdims=True) / width
+
+    def spread(idx, buf):
+        mine = buf.at[ds(k * rows + z * share_rows, share_rows), :]
+        along = [go(remote(mine, mine, zs.at[idx, i - 1], zr.at[idx, i - 1], ctx, zp(i))) for i in range(1, tps)]
+        across = [go(remote(mine, mine, ps.at[idx, 0], pr.at[idx, 0], partner, z))]
+
+        def finish():
+            for i in range(1, tps):
+                along[i - 1].wait_recv()
+                part = buf.at[ds(k * rows + ((z - i) % tps) * share_rows, share_rows), :]
+                across.append(go(remote(part, part, ps.at[idx, i], pr.at[idx, i], partner, z)))
+            for copy in across:
+                copy.wait_recv()
+
+        return finish
+
+    my_rows = ds(k * rows + z * share_rows, share_rows)
+    heads_rows = [None]
+
+    def o_partial(core, off):
+        left = att[pl.ds(core, 1)].reshape(rows, head_w)
+        return jnp.dot(left, w[3][:, ds(off, cw)], preferred_element_type=F32)
+
+    value = reduce_rows(0, o_partial, straight)
+    proj[...] = value
+    a_inverse = lax.rsqrt(mean_of(value * value) + EPS)
+    state = tok[my_rows, :].astype(F32) + value * a_inverse * gfull[0:1, :]
+    hstate[...] = state
+    hid[my_rows, :] = state.astype(BF16)
+    finish = spread(1, hid)
+    own_cot.wait()
+    for copy in cot_z:
+        copy.wait_recv()
+    att_t[...] = jnp.transpose(att[...].reshape(both, head_w))
+    finish()
+
+    fw = 256
+    for i, d in slots:
+        wait_w(4, i, d)
+
+    def gate_step(j, carry):
+        here = ds(j * fw, fw)
+        lin[:, here] = jnp.dot(hid[...], w[4][:, here], preferred_element_type=F32)
+        return carry
+
+    lax.fori_loop(0, ff_w // fw, gate_step, 0)
+    for s in range(width // 256):
+        hid_t[s * 256 : (s + 1) * 256, :] = jnp.transpose(hid[:, s * 256 : (s + 1) * 256])
+    for i, d in slots:
+        wait_w(5, i, d)
+
+    def up_step(j, carry):
+        here = ds(j * fw, fw)
+        up = jnp.dot(hid[...], w[5][:, here], preferred_element_type=F32)
+        gate = lin[:, here]
+        sigma = jax.nn.sigmoid(gate)
+        swish = gate * sigma
+        lin[:, here] = swish
+        fac[:, here] = up * sigma * (1.0 + gate * (1.0 - sigma))
+        value = (swish * up).astype(BF16)
+        act[:, here] = value
+        act_t[here, :] = jnp.transpose(value)
+        return carry
+
+    lax.fori_loop(0, ff_w // fw, up_step, 0)
+
+    def down_partial(core, off):
+        return jnp.dot(act[ds(core * rows, rows), :], w[6][:, ds(off, cw)], preferred_element_type=F32)
+
+    def from_chip(i):
+        return ((c - i) % chips) * cw
+
+    def down_ready(i):
+        wait_w(6, i, 0)
+        wait_w(6, i, 1)
+
+    value = reduce_rows(1, down_partial, from_chip, down_ready)
+    m_inverse = lax.rsqrt(mean_of(value * value) + EPS)
+    scaled = value * m_inverse
+    stage[...] = hstate[...] + scaled * gfull[1:2, :]
+    for i in range(1, tps):
+        go(remote(stage.at[:, ds(zp(i) * feats, feats)], out_ref.at[ds(z * share_rows, share_rows), :], ms.at[3, i - 1], mr.at[3, i - 1], ctx, zp(i)))
+    out_z = pending[-(tps - 1) :]
+    own_out = pltpu.make_async_copy(stage.at[:, ds(z * feats, feats)], out_ref.at[ds(z * share_rows, share_rows), :], loc.at[24])
+    own_out.start()
+    upstream = cot[...].astype(F32)
+    gained = upstream * gfull[1:2, :]
+    gg_row[1:2, :] = jnp.sum(upstream * scaled, axis=0, keepdims=True)
+    back_mix = m_inverse * gained - scaled * (m_inverse * m_inverse) * mean_of(gained * value)
+    dmix[my_rows, :] = back_mix.astype(BF16)
+    spread(2, dmix)()
+
+    def dact_step(j, carry):
+        here = ds(j * fw, fw)
+        d_act = lax.dot_general(dmix[...], w[6][here, :], NT, preferred_element_type=F32)
+        dup[:, here] = (d_act * lin[:, here]).astype(BF16)
+        dgate[:, here] = (d_act * fac[:, here]).astype(BF16)
+        return carry
+
+    lax.fori_loop(0, ff_w // fw, dact_step, 0)
+
+    def gdown_step(j, carry):
+        here = ds(j * fw, fw)
+        w[6][:, here] = jnp.dot(act_t[...], dmix[:, here], preferred_element_type=F32).astype(BF16)
+        return carry
+
+    lax.fori_loop(0, width // fw, gdown_step, 0)
+    send_g(6)
+
+    def ff_partial(core, off):
+        here = ds(core * rows, rows)
+        return lax.dot_general(dgate[here, :], w[4][ds(off, cw), :], NT, preferred_element_type=F32) + lax.dot_general(
+            dup[here, :], w[5][ds(off, cw), :], NT, preferred_element_type=F32
+        )
+
+    value = reduce_rows(2, ff_partial, straight) + cot[...].astype(F32)
+    dhid[...] = value
+    projected = proj[...]
+    a_inverse = lax.rsqrt(mean_of(projected * projected) + EPS)
+    scaled = projected * a_inverse
+    gained = value * gfull[0:1, :]
+    gg_row[0:1, :] = jnp.sum(value * scaled, axis=0, keepdims=True)
+    gg_row[2:8, :] = jnp.zeros((6, width), F32)
+    back_att = a_inverse * gained - scaled * (a_inverse * a_inverse) * mean_of(gained * projected)
+    dattn[my_rows, :] = back_att.astype(BF16)
+    finish = spread(3, dattn)
+    gains_z = []
+    for i in range(1, tps):
+        gains_z.append(go(remote(gg_row.at[:, ds(zp(i) * feats, feats)], gg_rx1.at[i - 1], ms.at[4, i - 1], mr.at[4, i - 1], ctx, zp(i))))
+
+    def ggate_step(j, carry):
+        here = ds(j * fw, fw)
+        w[4][:, here] = jnp.dot(hid_t[...], dgate[:, here], preferred_element_type=F32).astype(BF16)
+        return carry
+
+    lax.fori_loop(0, ff_w // fw, ggate_step, 0)
+    send_g(4, 0, 2)
+    finish()
+
+    value = lax.dot_general(dattn[...], w[3][...], NT, preferred_element_type=F32)
+    dh[...] = value.astype(BF16).reshape(2, seqs, blk, head_w)
+    pair = to_owner(2, dh, d_o, False)
+    send_g(4, 2, 3)
+
+    def go_step(j, carry):
+        here = ds(j * fw, fw)
+        w[3][:, here] = jnp.dot(att_t[...], dattn[:, here], preferred_element_type=F32).astype(BF16)
+        return carry
+
+    lax.fori_loop(0, width // fw, go_step, 0)
+    arrive(pair)
+    dk_acc[...] = jnp.zeros((total, HD), F32)
+    dv_acc[...] = jnp.zeros((total, HD), F32)
+
+    def unattend(i, carry):
+        here = ds(i * step, step)
+        q = qa[0, pl.ds(2 * i, 2)].reshape(step, HD)
+        d_out = d_o[pl.ds(2 * i, 2)].reshape(step, HD)
+        d_p = lax.dot_general(d_out, qa[2].reshape(total, HD), NT, preferred_element_type=F32)
+        delta = jnp.sum(d_out.astype(F32) * att_f[here, :], axis=1, keepdims=True)
+        p = probs[here, :]
+        d_s = (p.astype(F32) * (d_p - delta)).astype(BF16)
+        d_q = jnp.dot(d_s, qa[1].reshape(total, HD), preferred_element_type=F32) * scale
+        dqkv_st[0, pl.ds(2 * i, 2)] = d_q.astype(BF16).reshape(2, blk, HD)
+        dk_acc[...] += lax.dot_general(d_s, q, TN, preferred_element_type=F32)
+        dv_acc[...] += lax.dot_general(p, d_out, TN, preferred_element_type=F32)
+        return carry
+
+    lax.fori_loop(0, chips, unattend, 0)
+    dqkv_st[1] = (dk_acc[...] * scale).astype(BF16).reshape(2 * chips, blk, HD)
+    dqkv_st[2] = dv_acc[...].astype(BF16).reshape(2 * chips, blk, HD)
+    pair = from_owner(3, dqkv_st, dqkv, True)
+
+    def gup_step(j, carry):
+        here = ds(j * fw, fw)
+        w[5][:, here] = jnp.dot(hid_t[...], dup[:, here], preferred_element_type=F32).astype(BF16)
+        return carry
+
+    lax.fori_loop(0, ff_w // fw, gup_step, 0)
+    send_g(4, 3, 4)
+    send_g(5)
+    send_g(3)
+    arrive(pair)
+
+    gg_mid[...] = jnp.zeros((8, feats), F32)
+    for t, (raw, inv) in enumerate(((q_raw, inv_q), (k_raw, inv_k))):
+        folded = None
+        for h in range(heads):
+            lanes = slice(h * HD, (h + 1) * HD)
+            turned = dqkv[t, :, :, :, lanes].reshape(both, HD).astype(F32)
+            back_rot = turned * cosf[...] - pltpu.roll(turned, HD // 2, 1) * sinf[...]
+            plain = raw[:, lanes]
+            scaled = plain * inv[...]
+            gg_mid[2 + t : 3 + t, pl.ds(pl.multiple_of(k * head_w + h * HD, HD), HD)] = jnp.sum(back_rot * scaled, axis=0, keepdims=True)
+            gained = back_rot * gqk[t : t + 1, lanes]
+            dqkv[t, :, :, :, lanes] = gained.astype(BF16).reshape(2, seqs, blk, HD)
+            term = gained * plain
+            folded = term if folded is None else folded + term
+        sq_own[1, t : t + 1, :] = jnp.sum(jnp.transpose(folded), axis=0, keepdims=True)
+    sq_own[1, 2:8, :] = jnp.zeros((6, both), F32)
+    dots = totals(1) / width
+    for t, (raw, inv) in enumerate(((q_raw, inv_q), (k_raw, inv_k))):
+        spread_dot = column_of(dots[t : t + 1, :])
+        for h in range(heads):
+            lanes = slice(h * HD, (h + 1) * HD)
+            gained = dqkv[t, :, :, :, lanes].reshape(both, HD).astype(F32)
+            r = inv[...]
+            grad = r * gained - raw[:, lanes] * (r * r * r) * spread_dot
+            dqkv[t, :, :, :, lanes] = grad.astype(BF16).reshape(2, seqs, blk, HD)
+
+    def rf_copy(i, off):
+        return remote(st_z.at[:, ds(off, cw)], rx_f.at[i], rzs.at[3, i, 0], rzr.at[3, i, 0], ctx, zp(i + 1))
+
+    def in_partial(core, off):
+        here = ds(off, cw)
+        acc = None
+        for t in range(3):
+            left = dqkv[t, pl.ds(core, 1)].reshape(rows, head_w)
+            term = lax.dot_general(left, w[t][here, :], NT, preferred_element_type=F32)
+            acc = term if acc is None else acc + term
+        return acc
+
+    own_rows = ds(z * share_rows, share_rows)
+    for i in range(tps):
+        off = zp(i + 1) * cw
+        st_p[:, ds(off, cw)] = in_partial(ok, off).astype(BF16)
+        rp_copy(3, i, off).start()
+        mine = in_partial(k, off)
+        rp_copy(3, i, off).wait_recv()
+        st_z[:, ds(off, cw)] = (mine + rx_p[1, :, ds(off, cw)].astype(F32)).astype(BF16)
+        st_z[own_rows, ds(off, cw)] = (st_z[own_rows, ds(off, cw)].astype(F32) + dhid[:, ds(off, cw)]).astype(BF16)
+        if i < tps - 1:
+            rf_copy(i, off).start()
+
+    for m in range(3):
+
+        def gqkv_step(j, carry):
+            here = ds(j * 512, 512)
+            right = dqkv[m].reshape(both, head_w)
+            w[m][here, :] = jnp.dot(tok_t[here, :], right, preferred_element_type=F32).astype(BF16)
+            return carry
+
+        lax.fori_loop(0, width // 512, gqkv_step, 0)
+        send_g(m)
+    middle = gg_row[:, ds(z * feats, feats)]
+    for i, copy in enumerate(gains_z):
+        copy.wait_recv()
+        middle = middle + gg_rx1[i]
+    gg_mid[...] = gg_mid[...] + middle
+    gains_c = []
+    n = 0
+    for i, d in slots:
+        if i or d:
+            core = (k + d) % 2
+            gains_c.append(go(remote(gg_mid.at[:, ds(chip(i) * 128, 128)], gg_rx2.at[n], ms.at[5, n], mr.at[5, n], chip(i) * 2 + core, z)))
+            n += 1
+
+    for i in range(tps - 1):
+        rf_copy(i, zp(i + 1) * cw).wait_recv()
+    final = st_z[:, ds(z * feats, cw)].astype(F32)
+    for i in range(tps - 1):
+        final = final + rx_f[i].astype(F32)
+    gin_ref[...] = final
+    for i in range(tps):
+        rp_copy(3, i, zp(i + 1) * cw).wait_send()
+        if i < tps - 1:
+            rf_copy(i, zp(i + 1) * cw).wait_send()
+    gain_sum = gg_mid[:, ds(c * 128, 128)]
+    for i, copy in enumerate(gains_c):
+        copy.wait_recv()
+        gain_sum = gain_sum + gg_rx2[i]
+    ggain_ref[...] = gain_sum
+    own_out.wait()
+    for copy in out_z:
+        copy.wait_recv()
+    for copy in g_own:
+        copy.wait()
+    for copy in g_live:
+        copy.wait_recv()
+    for copy in pending:
+        copy.wait_send()
+
+
+def fused(
+    tokens,
+    w_query,
+    w_key,
+    w_value,
+    w_output,
+    w_gate,
+    w_up,
+    w_down,
+    gain_query,
+    gain_key,
+    gain_attention,
+    gain_feedforward,
+    block_order,
+    cotangent,
+):
+    seqs, blk, feats = tokens.shape
+    tps = lax.axis_size("tp")
+    chips = lax.axis_size("ctx") // 2
+    width = feats * tps
+    rows = seqs * blk
+    both = 2 * rows
+    share_rows = rows // tps
+    total = 2 * chips * blk
+    head_w = w_query.shape[1] // 2
+    ff_w = w_gate.shape[1] // 2
+    heads = head_w // HD
+    slab = width // (2 * chips)
+    ctx = lax.axis_index("ctx")
+    chip = ctx // 2
+    pair = lax.dynamic_slice_in_dim(block_order, 2 * chip, 2, 1)
+    inner = jnp.arange(blk, dtype=jnp.int32)
+    positions = (pair.T[:, :, None] * blk + inner).reshape(both)
+    frequency = THETA ** (-2.0 * jnp.arange(HD // 2, dtype=F32) / HD)
+    angles = positions.astype(F32)[:, None] * frequency
+    cosine, sine = jnp.cos(angles), jnp.sin(angles)
+    cosf = jnp.concatenate([cosine, cosine], axis=1)
+    sinf = jnp.concatenate([-sine, sine], axis=1)
+    mine = lax.dynamic_slice_in_dim(block_order, chip // heads, 1, 0)
+    order = (mine.reshape(-1, 1) * blk + inner).reshape(total)
+    pos_row = jnp.broadcast_to(order[None, :], (8, total))
+    pos_col = jnp.broadcast_to(order[:, None], (total, 128))
+    gains = jnp.stack([gain_query, gain_key, gain_attention, gain_feedforward]).astype(F32)
+    gains = jnp.pad(gains, ((0, 4), (0, 0)))
+    blank = jnp.zeros_like(gains)
+    gtile = jnp.where(ctx % 2 == 0, jnp.concatenate([gains, blank], axis=1), jnp.concatenate([blank, gains], axis=1))
+    weights = (w_query, w_key, w_value, w_output, w_gate, w_up, w_down)
+    dims = (chips, tps, seqs, blk, width, head_w, ff_w)
+    halves = (head_w, head_w, head_w, head_w, ff_w, ff_w, ff_w)
+    hbm = pl.BlockSpec(memory_space=pl.ANY)
+    vmem = pl.BlockSpec(memory_space=pltpu.VMEM)
+
+    def v(shape, dtype=BF16):
+        return pltpu.VMEM(shape, dtype)
+
+    w_shapes = [v((width, h)) if m in COLS else v((h, width)) for m, h in enumerate(halves)]
+    dma = pltpu.SemaphoreType.DMA
+    scratch = w_shapes + [
+        v((both, width)),
+        v((width, both)),
+        v((both, width)),
+        v((width, both)),
+        v((both, width)),
+        v((both, width)),
+        v((both, ff_w), F32),
+        v((both, ff_w), F32),
+        v((both, ff_w)),
+        v((ff_w, both)),
+        v((both, ff_w)),
+        v((both, ff_w)),
+        v((rows, width)),
+        v((2, rows, width)),
+        v((rows, width)),
+        v((2, tps - 1, share_rows, width)),
+        v((tps - 1, rows, feats)),
+        v((both, head_w), F32),
+        v((both, head_w), F32),
+        v((3, 2, seqs, blk, head_w)),
+        v((3, 2 * chips, blk, HD)),
+        v((total, total)),
+        v((total, HD), F32),
+        v((2 * chips, blk, HD)),
+        v((2, seqs, blk, head_w)),
+        v((head_w, both)),
+        v((2, seqs, blk, head_w)),
+        v((2 * chips, blk, HD)),
+        v((total, HD), F32),
+        v((total, HD), F32),
+        v((3, 2 * chips, blk, HD)),
+        v((3, 2, seqs, blk, head_w)),
+        v((2, 8, both), F32),
+        v((2, 2 * tps - 1, 8, both), F32),
+        v((both, 128), F32),
+        v((both, 128), F32),
+        v((share_rows, width)),
+        v((share_rows, width), F32),
+        v((share_rows, width), F32),
+        v((share_rows, width), F32),
+        v((share_rows, width), F32),
+        v((share_rows, width), F32),
+        v((2 * chips, 8, 128), F32),
+        v((tps, 2 * chips, 8, 128), F32),
+        v((8, width), F32),
+        v((8, head_w), F32),
+        v((8, width), F32),
+        v((tps - 1, 8, feats), F32),
+        v((8, feats), F32),
+        v((2 * chips - 1, 8, 128), F32),
+        dma((7, 2 * chips)),
+        dma((7, 2 * chips)),
+        dma((7, 2 * chips)),
+        dma((7, 2 * chips)),
+        dma((4, tps - 1)),
+        dma((4, tps - 1)),
+        dma((4, tps)),
+        dma((4, tps)),
+        dma((4, tps)),
+        dma((4, tps)),
+        dma((4, tps, tps - 1)),
+        dma((4, tps, tps - 1)),
+        dma((6, 2 * chips)),
+        dma((6, 2 * chips)),
+        dma((2, 2 * tps - 1)),
+        dma((2, 2 * tps - 1)),
+        dma((4, chips - 1)),
+        dma((4, chips - 1)),
+        dma((25,)),
+    ]
+    results = pl.pallas_call(
+        functools.partial(layer_kernel, dims),
+        out_shape=[
+            jax.ShapeDtypeStruct((rows, feats), F32),
+            jax.ShapeDtypeStruct((rows, feats), F32),
+            jax.ShapeDtypeStruct((8, 128), F32),
+        ]
+        + [jax.ShapeDtypeStruct((chips,) + weight.shape, BF16) for weight in weights],
+        in_specs=[hbm] * 9 + [vmem] * 5,
+        out_specs=[hbm, vmem, vmem] + [hbm] * 7,
+        scratch_shapes=scratch,
+        compiler_params=pltpu.CompilerParams(
+            collective_id=0, has_side_effects=True, vmem_limit_bytes=67043328
+        ),
+        name="layer",
+    )(tokens.reshape(rows, feats), cotangent.reshape(rows, feats), *weights, gtile, cosf, sinf, pos_row, pos_col)
+    output = results[0].reshape(tokens.shape)
+    grad_input = results[1].reshape(tokens.shape)
+    grads = [jnp.sum(received.astype(F32), axis=0) for received in results[3:]]
+    lanes = lax.dynamic_slice_in_dim(results[2], (ctx % 2) * 64, 64, 1)
+    return (output, grad_input, *grads, lanes[2], lanes[3], lanes[0], lanes[1])
+
+
+def fits(mesh):
+    return mesh.shape["ctx"] == 8 and mesh.shape["tp"] == 4
+
+
 def solution(mesh):
     placed = (
         P(None, "ctx", "tp"),
@@ -421,7 +1227,7 @@
         P(None, "ctx", "tp"),
     )
     return jax.shard_map(
-        shards,
+        fused if fits(mesh) else shards,
         mesh=mesh,
         in_specs=placed,
         out_specs=(

time: 1240 us -> 491 us (0.40)
  waiting for transfers between devices: 895 us -> 0 us
  Pallas kernels: 0 us -> 463 us
  matrix products: 124 us -> 0 us
  blocking collectives: 91.2 us -> 0 us
  local copies, waits for them, and re-layouts: 52 us -> 6.33 us
  other arithmetic: 47.4 us -> 17.8 us
  between operations: 16.3 us -> 0.74 us
    reduce_scatter x11 -> x0, waiting for transfers between devices: 511 us -> none  [the longest x4 174 us: share(): return lax.psum_scatter(value, 'tp', scatter_dimension=2, tiled=True)]
    pallas_call x0 -> x1, Pallas kernels: none -> 463 us  [fused(): pl.pallas_call(functools.partial(layer_kernel, dims), out_shape=[jax.Shap...]
    all_gather x13 -> x0, waiting for transfers between devices: 377 us -> none  [the longest x4 83.1 us: full_width(): return lax.all_gather(value, 'tp', axis=2, tiled=True)]
    dot_general x35 -> x0, matrix products: 124 us -> none  [the longest x2 8.22 us: query_span(): jnp.einsum('shqk,skhd->sqhd', d_scores, key_piece, preferred_element_type...]
    psum x6 -> x0, blocking collectives: 62.6 us -> none  [tp_total(): return lax.psum(values, 'tp')]
    unnamed x2 -> x0, blocking collectives: 28.6 us -> none
    unnamed x112 -> x16, local copies, waits for them, and re-layouts: 26.7 us -> 3.25 us
    convert_element_type x19 -> x1, other arithmetic: 20.6 us -> 0.07 us  [fused(): angles = positions.astype(F32)[:, None] * frequency]
  transfers between devices with their start and end apart: 25 -> 0, of which waited for: 25 -> 0; matrix products, arithmetic and copies ran while one was open for 11% -> 0% of each run, Pallas kernels for 0% -> 0%
where the time goes in v1:
time: 491 us; the launch traced here: 488 us
  Pallas kernels  463 us (94%)
  other arithmetic  17.8 us (4%)
  local copies, waits for them, and re-layouts  6.33 us (1%)
    pallas_call x1, Pallas kernels, fused(): pl.pallas_call(functools.partial(layer_kernel, dims), out_shape=[jax.Shap...  463 us
    reduce_sum x7, other arithmetic, fused(): grads = [jnp.sum(received.astype(F32), axis=0) for received in results[3:]]  12.8 us

profile of v1, /device:TPU:0, one launch (start us, length us, event | category | flops | bytes accessed | tf_op | source)
XLA Modules:
  0.0 488.0 jit_solution(7660362471507467922)
XLA Ops:
  0.7 0.7 fusion.10
  1.4 0.8 multiply_bitcast_fusion
  2.1 0.1 copy.27
  2.2 0.1 add_convert_fusion
  2.3 0.1 add_bitcast_fusion
  2.4 0.7 fusion.8
  3.1 0.7 pad_select_fusion.refs_9_
  3.8 0.6 broadcast_in_dim.4.refs_12_
  4.4 1.0 broadcast_in_dim.5.refs_13_
  5.4 1.0 fusion
  6.4 1.0 pad_maximum_fusion
  7.4 463.2 %layer.1 = (f32[256,512]{1,0:T(8,128)}, f32[256,512]{1,0:T(8,128)}, f32[8,128]{1,0:T(8,128)}, bf16[4,256,512]{2,1,0:T(8,128)(2,1)}, bf16[4,256,512]{2,1,0:T(8,12...) custom-call(bf16[256,512]{1,0:T(8,128)(2,1)} %bitcast.25, ...), custom_call_target="tpu_custom_call" | custom-call | tf_op jit(solution)/shard_map/layer/pallas_call | solution.py:1185
  470.6 0.0 copy-start.4
  470.6 0.8 constant_dynamic-slice_fusion
  471.4 0.5 slice_bitcast_fusion
  472.0 0.0 copy-start.3
  472.0 2.3 convert_reduce_fusion.6
  474.3 0.0 copy-start.2
  474.3 2.4 convert_reduce_fusion.5
  476.6 0.0 copy-done.4
  476.6 0.9 convert_reduce_fusion.4
  477.6 0.0 copy-done.3
  477.6 0.9 convert_reduce_fusion.3
  478.5 0.0 copy-done.2
  478.5 0.0 copy-start.1
  478.5 2.1 convert_reduce_fusion.2
  480.6 0.8 copy-done.1
  481.4 0.0 copy-start
  481.5 2.1 convert_reduce_fusion.1
  483.6 0.8 copy-done
  484.4 0.0 copy-start.6
  484.4 0.0 copy-start.5
  484.4 2.0 convert_reduce_fusion
  486.4 0.0 copy-done.6
  486.4 0.8 copy.30
  487.2 0.0 copy-done.5
  487.2 0.8 copy.31
  (1 shorter events, 0.0 us)
Async XLA Ops:
  470.6 6.1 %copy-start.4 = (bf16[4,256,512]{2,1,0:T(8,128)(2,1)S(1)}, bf16[4,256,512]{2,1,0:T(8,128)(2,1)}, u32[]{:S(2)}) copy-start(bf16[4,256,512]{2,1,0:T(8,128)(2,1)} %get-tuple-element.27) | copy-start | bytes 3145732
  472.0 5.6 %copy-start.3 = (bf16[4,512,256]{2,1,0:T(8,128)(2,1)S(1)}, bf16[4,512,256]{2,1,0:T(8,128)(2,1)}, u32[]{:S(2)}) copy-start(bf16[4,512,256]{2,1,0:T(8,128)(2,1)} %get-tuple-element.28) | copy-start | bytes 3145732
  474.3 4.2 copy-start.2
  478.5 2.9 copy-start.1
  481.4 2.9 copy-start
  484.4 2.0 copy-start.6
  484.4 2.8 copy-start.5

commit v2 on v1

--- a/solution.py
+++ b/solution.py
@@ -437,13 +437,14 @@
     (out_ref, gin_ref, ggain_ref) = take(3)
     rx_g = take(7)
     w = take(7)
+    via = take(7)
     (tok, tok_t, hid, hid_t, dmix, dattn) = take(6)
     (lin, fac, act, act_t, dgate, dup) = take(6)
     (st_p, rx_p, st_z, rx_z, rx_f) = take(5)
     (q_raw, k_raw, qkv, qa, probs, att_f, att_st, att, att_t) = take(9)
     (dh, d_o, dk_acc, dv_acc, dqkv_st, dqkv) = take(6)
     (sq_own, sq_rx, inv_q, inv_k) = take(4)
-    (cot, proj, hstate, mixed, dhid, stage) = take(6)
+    (cot, proj, hstate, dhid, stage) = take(5)
     (gbuf, gall, gfull, gqk, gg_row, gg_rx1, gg_mid, gg_rx2) = take(8)
     (ws, wr, gs, gr) = take(4)
     (zs, zr, ps, pr) = take(4)
@@ -459,6 +460,8 @@
     k = ctx % 2
     ok = 1 - k
     partner = c * 2 + ok
+    near = (c + 1 - 2 * (c % 2), (c + 2) % chips)
+    far = chips - 1 - c
 
     def zp(i):
         return (z + i) % tps
@@ -493,59 +496,94 @@
         pending.append(copy)
         return copy
 
-    def w_copy(m, i, d):
+    def slab_of(m, owner):
+        if m in COLS:
+            return w[m].at[ds(owner * slab, slab), :]
+        return w[m].at[:, ds(owner * slab, slab)]
+
+    def half_of(m, core):
+        if m in COLS:
+            return w_in[m].at[:, ds(core * halves[m], halves[m])]
+        return w_in[m].at[ds(core * halves[m], halves[m]), :]
+
+    w_own = {}
+    w_pass = {}
+    w_wait = {}
+
+    def w_slot(m, n, owner):
+        return remote(slab_of(m, owner), slab_of(m, owner), ws.at[m, n], wr.at[m, n], partner, z)
+
+    def send_w(m, d):
         core = (k + d) % 2
-        half = halves[m]
+        for n in range(2):
+            go(remote(half_of(m, core), slab_of(m, ctx), ws.at[m, 2 * n + d], wr.at[m, 2 * n + k], near[n] * 2 + core, z))
+        if d:
+            go(remote(half_of(m, ok), slab_of(m, ctx), ws.at[m, 4], wr.at[m, 4], partner, z))
+        else:
+            w_own[m] = pltpu.make_async_copy(half_of(m, k), slab_of(m, ctx), loc.at[m])
+            w_own[m].start()
+
+    def source(n):
+        if n < 4:
+            return near[n // 2] * 2 + n % 2
+        return partner if n == 4 else far * 2 + n - 5
+
+    def got_w(m, *which):
+        for n in which:
+            if (m, n) not in w_wait:
+                w_wait[m, n] = True
+                w_slot(m, n, source(n)).wait_recv()
+
+    def pass_w(m):
+        for n in range(2):
+            got_w(m, 3 * n)
+            mine = slab_of(m, source(3 * n))
+            copy = remote(mine, mine, ws.at[m, 5 + n], wr.at[m, 5 + n], near[1 - n] * 2 + k, z)
+            copy.start()
+            w_pass[m, n] = copy
+
+    def free_w(m):
+        for n in range(2):
+            w_pass[m, n].wait_send()
+
+    def wait_w(m):
+        w_own[m].wait()
+        got_w(m, *range(7))
+
+    def into(m, n, core):
         if m in COLS:
-            src = w_in[m].at[:, ds(core * half, half)]
-            dst = w[m].at[ds(ctx * slab, slab), :]
-        else:
-            src = w_in[m].at[ds(core * half, half), :]
-            dst = w[m].at[:, ds(ctx * slab, slab)]
-        if i == 0 and d == 0:
-            return pltpu.make_async_copy(src, dst, loc.at[m])
-        return remote(src, dst, ws.at[m, 2 * i + d], wr.at[m, 2 * i + d], chip(i) * 2 + core, z)
-
-    slots = [(i, d) for i in range(chips) for d in range(2)]
-    w_live = {}
-
-    def send_w(m):
-        for i, d in slots:
-            copy = w_copy(m, i, d)
-            copy.start()
-            w_live[m, i, d] = copy
-            if i or d:
-                pending.append(copy)
-
-    def wait_w(m, i, d):
-        copy = w_live[m, i, d]
-        if i or d:
-            copy.wait_recv()
-        else:
-            copy.wait()
-
-    def send_g(m, chips_from=0, chips_to=chips):
-        half = halves[m]
-        for i in range(chips_from, chips_to):
-            for d in range(2):
-                to = chip(i) * 2 + (k + d) % 2
-                if m in COLS:
-                    src = w[m].at[ds(to * slab, slab), :]
-                    dst = rx_g[m].at[i, :, ds(k * half, half)]
-                else:
-                    src = w[m].at[:, ds(to * slab, slab)]
-                    dst = rx_g[m].at[i, ds(k * half, half), :]
-                if i or d:
-                    copy = remote(src, dst, gs.at[m, 2 * i + d], gr.at[m, 2 * i + d], to, z)
-                    go(copy)
-                    g_live.append(copy)
-                else:
-                    copy = pltpu.make_async_copy(src, dst, loc.at[8 + m])
-                    copy.start()
-                    g_own.append(copy)
+            return rx_g[m].at[n, :, ds(core * halves[m], halves[m])]
+        return rx_g[m].at[n, ds(core * halves[m], halves[m]), :]
 
     g_live = []
     g_own = []
+
+    def send_g(m):
+        for n in range(2):
+            go(remote(slab_of(m, far * 2 + n), via[m].at[n], gs.at[m, n], gr.at[m, n], near[n] * 2 + k, z))
+        for n in range(2):
+            go(remote(slab_of(m, near[n] * 2 + n), into(m, 1 + n, k), gs.at[m, 2 + n], gr.at[m, 2 + 2 * n + k], near[n] * 2 + n, z))
+        go(remote(slab_of(m, partner), into(m, 0, k), gs.at[m, 6], gr.at[m, 6], partner, z))
+        copy = pltpu.make_async_copy(slab_of(m, ctx), into(m, 0, k), loc.at[8 + m])
+        copy.start()
+        g_own.append(copy)
+
+    def pass_g(m):
+        for n in range(2):
+            to = near[1 - n] * 2 + n
+            remote(via[m].at[n], via[m].at[n], gs.at[m, n], gr.at[m, n], partner, z).wait_recv()
+            total = slab_of(m, to)[...].astype(F32) + via[m][n].astype(F32)
+            slab_of(m, to)[...] = total.astype(BF16)
+            go(remote(slab_of(m, to), into(m, 2 - n, k), gs.at[m, 4 + n], gr.at[m, 2 + 2 * (1 - n) + k], to, z))
+        g_live.append(m)
+
+    def wait_g(m):
+        for n in range(2):
+            for core in range(2):
+                here = into(m, 1 + n, core)
+                remote(here, here, gs.at[m, 0], gr.at[m, 2 + 2 * n + core], partner, z).wait_recv()
+        here = into(m, 0, ok)
+        remote(here, here, gs.at[m, 6], gr.at[m, 6], partner, z).wait_recv()
 
     own_tok = pltpu.make_async_copy(tok_in, tok.at[ds(k * rows, rows), ds(z * feats, feats)], loc.at[16])
     own_tok.start()
@@ -559,6 +597,7 @@
     for i in range(1, tps):
         tok_z.append(go(remote(tok_in, tok.at[ds(k * rows, rows), ds(z * feats, feats)], zs.at[0, i - 1], zr.at[0, i - 1], ctx, zp(i))))
     tok_p = [go(remote(tok_in, tok.at[ds(k * rows, rows), ds(z * feats, feats)], ps.at[0, 0], pr.at[0, 0], partner, z))]
+    slots = [(i, d) for i in range(chips) for d in range(2)]
     gain1 = []
     n = 0
     for i, d in slots:
@@ -569,7 +608,8 @@
     for i in range(1, tps):
         cot_z.append(go(remote(cot_in.at[ds(zp(i) * share_rows, share_rows), :], cot.at[:, ds(z * feats, feats)], ms.at[1, i - 1], mr.at[1, i - 1], ctx, zp(i))))
     for m in (0, 1, 2, 3):
-        send_w(m)
+        send_w(m, 0)
+        send_w(m, 1)
 
     own_gain.wait()
     for copy in gain1:
@@ -588,15 +628,9 @@
         tok_z[i - 1].wait_recv()
         part = tok.at[ds(k * rows, rows), ds(((z - i) % tps) * feats, feats)]
         tok_p.append(go(remote(part, part, ps.at[0, i], pr.at[0, i], partner, z)))
-    own_gain2.wait()
-    for copy in gain2:
-        copy.wait_recv()
-    for r in range(2):
-        pieces = []
-        for zz in range(tps):
-            for m in range(chips):
-                pieces.append(gall[zz, 2 * m, 2 + r : 3 + r, :] + gall[zz, 2 * m + 1, 2 + r : 3 + r, :])
-        gfull[r : r + 1, :] = jnp.concatenate(pieces, axis=1)
+    for m in (0, 1, 2, 3):
+        pass_w(m)
+    send_w(4, 0)
     for copy in tok_p:
         copy.wait_recv()
 
@@ -625,8 +659,7 @@
         return total
 
     for m in (0, 1, 2):
-        for i, d in slots:
-            wait_w(m, i, d)
+        wait_w(m)
         value = jnp.dot(tok[...], w[m][...], preferred_element_type=F32)
         if m == 0:
             q_raw[...] = value
@@ -634,7 +667,6 @@
         elif m == 1:
             k_raw[...] = value
             sq_own[0, 1:2, :] = row_of(value * value)
-            squares = None
         else:
             qkv[2] = value.astype(BF16).reshape(2, seqs, blk, head_w)
     sq_own[0, 2:8, :] = jnp.zeros((6, both), F32)
@@ -691,7 +723,9 @@
         for copy in copies:
             copy.wait_recv()
 
-    arrive(to_owner(0, qkv, qa, True))
+    pair = to_owner(0, qkv, qa, True)
+    send_w(4, 1)
+    arrive(pair)
     step = 2 * blk
 
     def attend(i, carry):
@@ -711,13 +745,23 @@
 
     lax.fori_loop(0, chips, attend, 0)
     back = from_owner(1, att_st, att, False)
-    for m in (4, 5, 6):
-        send_w(m)
+    pass_w(4)
+    for m in (5, 6):
+        send_w(m, 0)
+        send_w(m, 1)
+    own_gain2.wait()
+    for copy in gain2:
+        copy.wait_recv()
+    for r in range(2):
+        pieces = []
+        for zz in range(tps):
+            for m in range(chips):
+                pieces.append(gall[zz, 2 * m, 2 + r : 3 + r, :] + gall[zz, 2 * m + 1, 2 + r : 3 + r, :])
+        gfull[r : r + 1, :] = jnp.concatenate(pieces, axis=1)
     for s in range(width // 256):
         tok_t[s * 256 : (s + 1) * 256, :] = jnp.transpose(tok[:, s * 256 : (s + 1) * 256])
     arrive(back)
-    for i, d in slots:
-        wait_w(3, i, d)
+    wait_w(3)
 
     cw = feats
     rs_live = {}
@@ -735,7 +779,7 @@
             zp(j),
         )
 
-    def reduce_rows(idx, partial, offset, before=None):
+    def reduce_rows(idx, partial, offset, before=None, meanwhile=None):
         def one(i):
             off = offset(i)
             if before is not None:
@@ -760,7 +804,13 @@
         else:
             for i in range(tps):
                 one(i)
-        lax.fori_loop(0, tps, lambda i, x: (finish(i), x)[1], 0)
+        if meanwhile is not None:
+            meanwhile()
+        if before is None:
+            lax.fori_loop(0, tps, lambda i, x: (finish(i), x)[1], 0)
+        else:
+            for i in range(tps):
+                finish(i)
         mine = st_z[ds(z * share_rows, share_rows), :].astype(F32)
         for j in range(tps - 1):
             mine = mine + rx_z[idx % 2, j].astype(F32)
@@ -808,8 +858,8 @@
     finish()
 
     fw = 256
-    for i, d in slots:
-        wait_w(4, i, d)
+    pass_w(5)
+    wait_w(4)
 
     def gate_step(j, carry):
         here = ds(j * fw, fw)
@@ -819,8 +869,8 @@
     lax.fori_loop(0, ff_w // fw, gate_step, 0)
     for s in range(width // 256):
         hid_t[s * 256 : (s + 1) * 256, :] = jnp.transpose(hid[:, s * 256 : (s + 1) * 256])
-    for i, d in slots:
-        wait_w(5, i, d)
+    pass_w(6)
+    wait_w(5)
 
     def up_step(j, carry):
         here = ds(j * fw, fw)
@@ -841,11 +891,12 @@
         return jnp.dot(act[ds(core * rows, rows), :], w[6][:, ds(off, cw)], preferred_element_type=F32)
 
     def from_chip(i):
-        return ((c - i) % chips) * cw
+        return (c, near[0], near[1], far)[i] * cw
 
     def down_ready(i):
-        wait_w(6, i, 0)
-        wait_w(6, i, 1)
+        if i == 0:
+            w_own[6].wait()
+        got_w(6, *((4,), (0, 1), (2, 3), (5, 6))[i])
 
     value = reduce_rows(1, down_partial, from_chip, down_ready)
     m_inverse = lax.rsqrt(mean_of(value * value) + EPS)
@@ -877,6 +928,7 @@
         w[6][:, here] = jnp.dot(act_t[...], dmix[:, here], preferred_element_type=F32).astype(BF16)
         return carry
 
+    free_w(6)
     lax.fori_loop(0, width // fw, gdown_step, 0)
     send_g(6)
 
@@ -886,7 +938,18 @@
             dup[here, :], w[5][ds(off, cw), :], NT, preferred_element_type=F32
         )
 
-    value = reduce_rows(2, ff_partial, straight) + cot[...].astype(F32)
+    def ggate_step(j, carry):
+        here = ds(j * fw, fw)
+        w[4][:, here] = jnp.dot(hid_t[...], dgate[:, here], preferred_element_type=F32).astype(BF16)
+        return carry
+
+    def gate_grad():
+        free_w(4)
+        lax.fori_loop(0, ff_w // fw, ggate_step, 0)
+        pass_g(6)
+        send_g(4)
+
+    value = reduce_rows(2, ff_partial, straight, meanwhile=gate_grad) + cot[...].astype(F32)
     dhid[...] = value
     projected = proj[...]
     a_inverse = lax.rsqrt(mean_of(projected * projected) + EPS)
@@ -901,25 +964,26 @@
     for i in range(1, tps):
         gains_z.append(go(remote(gg_row.at[:, ds(zp(i) * feats, feats)], gg_rx1.at[i - 1], ms.at[4, i - 1], mr.at[4, i - 1], ctx, zp(i))))
 
-    def ggate_step(j, carry):
+    def gup_step(j, carry):
         here = ds(j * fw, fw)
-        w[4][:, here] = jnp.dot(hid_t[...], dgate[:, here], preferred_element_type=F32).astype(BF16)
+        w[5][:, here] = jnp.dot(hid_t[...], dup[:, here], preferred_element_type=F32).astype(BF16)
         return carry
 
-    lax.fori_loop(0, ff_w // fw, ggate_step, 0)
-    send_g(4, 0, 2)
+    free_w(5)
+    lax.fori_loop(0, ff_w // fw, gup_step, 0)
     finish()
 
     value = lax.dot_general(dattn[...], w[3][...], NT, preferred_element_type=F32)
     dh[...] = value.astype(BF16).reshape(2, seqs, blk, head_w)
     pair = to_owner(2, dh, d_o, False)
-    send_g(4, 2, 3)
+    pass_g(4)
 
     def go_step(j, carry):
         here = ds(j * fw, fw)
         w[3][:, here] = jnp.dot(att_t[...], dattn[:, here], preferred_element_type=F32).astype(BF16)
         return carry
 
+    free_w(3)
     lax.fori_loop(0, width // fw, go_step, 0)
     arrive(pair)
     dk_acc[...] = jnp.zeros((total, HD), F32)
@@ -944,13 +1008,6 @@
     dqkv_st[2] = dv_acc[...].astype(BF16).reshape(2 * chips, blk, HD)
     pair = from_owner(3, dqkv_st, dqkv, True)
 
-    def gup_step(j, carry):
-        here = ds(j * fw, fw)
-        w[5][:, here] = jnp.dot(hid_t[...], dup[:, here], preferred_element_type=F32).astype(BF16)
-        return carry
-
-    lax.fori_loop(0, ff_w // fw, gup_step, 0)
-    send_g(4, 3, 4)
     send_g(5)
     send_g(3)
     arrive(pair)
@@ -1005,6 +1062,8 @@
         if i < tps - 1:
             rf_copy(i, off).start()
 
+    pass_g(5)
+    pass_g(3)
     for m in range(3):
 
         def gqkv_step(j, carry):
@@ -1013,6 +1072,7 @@
             w[m][here, :] = jnp.dot(tok_t[here, :], right, preferred_element_type=F32).astype(BF16)
             return carry
 
+        free_w(m)
         lax.fori_loop(0, width // 512, gqkv_step, 0)
         send_g(m)
     middle = gg_row[:, ds(z * feats, feats)]
@@ -1028,6 +1088,8 @@
             gains_c.append(go(remote(gg_mid.at[:, ds(chip(i) * 128, 128)], gg_rx2.at[n], ms.at[5, n], mr.at[5, n], chip(i) * 2 + core, z)))
             n += 1
 
+    for m in range(3):
+        pass_g(m)
     for i in range(tps - 1):
         rf_copy(i, zp(i + 1) * cw).wait_recv()
     final = st_z[:, ds(z * feats, cw)].astype(F32)
@@ -1048,8 +1110,8 @@
         copy.wait_recv()
     for copy in g_own:
         copy.wait()
-    for copy in g_live:
-        copy.wait_recv()
+    for m in g_live:
+        wait_g(m)
     for copy in pending:
         copy.wait_send()
 
@@ -1111,7 +1173,8 @@
 
     w_shapes = [v((width, h)) if m in COLS else v((h, width)) for m, h in enumerate(halves)]
     dma = pltpu.SemaphoreType.DMA
-    scratch = w_shapes + [
+    v_shapes = [v((2, slab, h)) if m in COLS else v((2, h, slab)) for m, h in enumerate(halves)]
+    scratch = w_shapes + v_shapes + [
         v((both, width)),
         v((width, both)),
         v((both, width)),
@@ -1153,7 +1216,6 @@
         v((share_rows, width), F32),
         v((share_rows, width), F32),
         v((share_rows, width), F32),
-        v((share_rows, width), F32),
         v((2 * chips, 8, 128), F32),
         v((tps, 2 * chips, 8, 128), F32),
         v((8, width), F32),
@@ -1189,7 +1251,7 @@
             jax.ShapeDtypeStruct((rows, feats), F32),
             jax.ShapeDtypeStruct((8, 128), F32),
         ]
-        + [jax.ShapeDtypeStruct((chips,) + weight.shape, BF16) for weight in weights],
+        + [jax.ShapeDtypeStruct((3,) + weight.shape, BF16) for weight in weights],
         in_specs=[hbm] * 9 + [vmem] * 5,
         out_specs=[hbm, vmem, vmem] + [hbm] * 7,
         scratch_shapes=scratch,

time: 491 us -> 396 us (0.81)
  Pallas kernels: 463 us -> 369 us
    pallas_call x1, Pallas kernels: 463 us -> 369 us  [fused(): pl.pallas_call(functools.partial(layer_kernel, dims), out_shape=[jax.Shap...]
where the time goes in v2:
time: 396 us; the launch traced here: 393 us
  Pallas kernels  369 us (93%)
  other arithmetic  16.7 us (4%)
  local copies, waits for them, and re-layouts  5.99 us (2%)
    pallas_call x1, Pallas kernels, fused(): pl.pallas_call(functools.partial(layer_kernel, dims), out_shape=[jax.Shap...  369 us
    reduce_sum x7, other arithmetic, fused(): grads = [jnp.sum(received.astype(F32), axis=0) for received in results[3:]]  11.8 us

profile of v2, /device:TPU:0, one launch (start us, length us, event | category | flops | bytes accessed | tf_op | source)
XLA Modules:
  0.0 392.8 jit_solution(160319776649882697)
XLA Ops:
  0.7 0.7 fusion.10
  1.4 0.8 multiply_bitcast_fusion
  2.1 0.1 copy.27
  2.2 0.1 add_convert_fusion
  2.3 0.1 add_bitcast_fusion
  2.4 0.7 fusion.8
  3.1 0.7 pad_select_fusion.refs_9_
  3.8 0.6 broadcast_in_dim.4.refs_12_
  4.4 1.0 broadcast_in_dim.5.refs_13_
  5.4 1.0 fusion
  6.4 1.0 pad_maximum_fusion
  7.4 369.3 %layer.1 = (f32[256,512]{1,0:T(8,128)}, f32[256,512]{1,0:T(8,128)}, f32[8,128]{1,0:T(8,128)}, bf16[3,256,512]{2,1,0:T(8,128)(2,1)}, bf16[3,256,512]{2,1,0:T(8,12...) custom-call(bf16[256,512]{1,0:T(8,128)(2,1)} %bitcast.25, ...), custom_call_target="tpu_custom_call" | custom-call | tf_op jit(solution)/shard_map/layer/pallas_call | solution.py:1247
  376.7 0.0 copy-start.4
  376.8 0.0 copy-start.3
  376.8 0.9 constant_dynamic-slice_fusion
  377.6 0.5 slice_bitcast_fusion
  378.2 2.1 convert_reduce_fusion.6
  380.2 0.0 copy-start.2
  380.3 2.2 convert_reduce_fusion.5
  382.5 0.0 copy-done.4
  382.5 0.9 convert_reduce_fusion.4
  383.4 0.0 copy-done.3
  383.4 0.9 convert_reduce_fusion.3
  384.3 0.0 copy-done.2
  384.3 0.0 copy-start.1
  384.3 2.0 convert_reduce_fusion.2
  386.3 0.6 copy-done.1
  386.9 0.0 copy-start
  386.9 2.0 convert_reduce_fusion.1
  388.9 0.6 copy-done
  389.5 0.0 copy-start.6
  389.5 0.0 copy-start.5
  389.5 1.7 convert_reduce_fusion
  391.2 0.0 copy-done.6
  391.2 0.8 copy.30
  392.0 0.0 copy-done.5
  392.0 0.8 copy.31
  (1 shorter events, 0.0 us)
Async XLA Ops:
  376.7 5.8 %copy-start.4 = (bf16[3,256,512]{2,1,0:T(8,128)(2,1)S(1)}, bf16[3,256,512]{2,1,0:T(8,128)(2,1)}, u32[]{:S(2)}) copy-start(bf16[3,256,512]{2,1,0:T(8,128)(2,1)} %get-tuple-element.27) | copy-start | bytes 2359300
  376.8 6.6 %copy-start.3 = (bf16[3,512,256]{2,1,0:T(8,128)(2,1)S(1)}, bf16[3,512,256]{2,1,0:T(8,128)(2,1)}, u32[]{:S(2)}) copy-start(bf16[3,512,256]{2,1,0:T(8,128)(2,1)} %get-tuple-element.28) | copy-start | bytes 2359300
  380.2 4.0 %copy-start.2 = (bf16[3,256,2048]{2,1,0:T(8,128)(2,1)S(1)}, bf16[3,256,2048]{2,1,0:T(8,128)(2,1)}, u32[]{:S(2)}) copy-start(bf16[3,256,2048]{2,1,0:T(8,128)(2,1)} %get-tuple-element.29) | copy-start | bytes 9437188
  384.3 2.6 copy-start.1
  386.9 2.6 copy-start
  389.5 1.7 copy-start.6
  389.5 2.5 copy-start.5

commit v3 on v2

--- a/solution.py
+++ b/solution.py
@@ -2,6 +2,7 @@
 
 import jax
 import jax.numpy as jnp
+import numpy as np
 from jax import lax
 from jax.experimental import pallas as pl
 from jax.experimental.pallas import tpu as pltpu
@@ -433,7 +434,7 @@
 
     (tok_in, cot_in) = take(2)
     w_in = take(7)
-    (gtile, cosf, sinf, pos_row, pos_col) = take(5)
+    (blocks, gtile, table) = take(3)
     (out_ref, gin_ref, ggain_ref) = take(3)
     rx_g = take(7)
     w = take(7)
@@ -442,7 +443,7 @@
     (lin, fac, act, act_t, dgate, dup) = take(6)
     (st_p, rx_p, st_z, rx_z, rx_f) = take(5)
     (q_raw, k_raw, qkv, qa, probs, att_f, att_st, att, att_t) = take(9)
-    (dh, d_o, dk_acc, dv_acc, dqkv_st, dqkv) = take(6)
+    (dh, d_o, dqkv_st, dqkv) = take(4)
     (sq_own, sq_rx, inv_q, inv_k) = take(4)
     (cot, proj, hstate, dhid, stage) = take(5)
     (gbuf, gall, gfull, gqk, gg_row, gg_rx1, gg_mid, gg_rx2) = take(8)
@@ -453,6 +454,8 @@
     (ss, sr) = take(2)
     (as_, ar) = take(2)
     (loc,) = take(1)
+    (d_acc, cosf, sinf, pos_row) = take(4)
+    (xs, xr) = take(2)
 
     ctx = lax.axis_index("ctx")
     z = lax.axis_index("tp")
@@ -558,15 +561,24 @@
     g_live = []
     g_own = []
 
-    def send_g(m):
+    def send_far(m):
         for n in range(2):
             go(remote(slab_of(m, far * 2 + n), via[m].at[n], gs.at[m, n], gr.at[m, n], near[n] * 2 + k, z))
-        for n in range(2):
-            go(remote(slab_of(m, near[n] * 2 + n), into(m, 1 + n, k), gs.at[m, 2 + n], gr.at[m, 2 + 2 * n + k], near[n] * 2 + n, z))
+
+    def send_near(m, n):
+        go(remote(slab_of(m, near[n] * 2 + n), into(m, 1 + n, k), gs.at[m, 2 + n], gr.at[m, 2 + 2 * n + k], near[n] * 2 + n, z))
+
+    def send_home(m):
         go(remote(slab_of(m, partner), into(m, 0, k), gs.at[m, 6], gr.at[m, 6], partner, z))
         copy = pltpu.make_async_copy(slab_of(m, ctx), into(m, 0, k), loc.at[8 + m])
         copy.start()
         g_own.append(copy)
+
+    def send_g(m):
+        send_far(m)
+        send_near(m, 0)
+        send_near(m, 1)
+        send_home(m)
 
     def pass_g(m):
         for n in range(2):
@@ -622,6 +634,21 @@
     for r in range(2):
         pieces = [gbuf[4 * k + 2 * m, r : r + 1, :] + gbuf[4 * k + 2 * m + 1, r : r + 1, :] for m in range(head_w // 128)]
         gqk[r : r + 1, :] = jnp.concatenate(pieces, axis=1)
+
+    lane = lax.broadcasted_iota(jnp.int32, (blk, HD), 1)
+    sign = jnp.where(lane < HD // 2, -1.0, 1.0)
+    for core in range(2):
+        for s in range(seqs):
+            block = blocks[s, 2 * c + core]
+            c_block, s_block = table[0, pl.ds(block, 1), :], table[1, pl.ds(block, 1), :]
+            c_in, s_in = table[2], table[3]
+            here = slice((core * seqs + s) * blk, (core * seqs + s + 1) * blk)
+            cosf[here, :] = c_block * c_in - s_block * s_in
+            sinf[here, :] = (s_block * c_in + c_block * s_in) * sign
+    for j in range(2 * chips):
+        start = blocks[c // heads, j] * blk
+        here = slice(j * blk, (j + 1) * blk)
+        pos_row[:, here] = start + lane[0:8, :]
 
     own_tok.wait()
     for i in range(1, tps):
@@ -732,7 +759,10 @@
         here = ds(i * step, step)
         q = qa[0, pl.ds(2 * i, 2)].reshape(step, HD)
         s = lax.dot_general(q, qa[1].reshape(total, HD), NT, preferred_element_type=F32) * scale
-        visible = pos_row[0:1, :] <= pos_col[here, 0:1]
+        at = lax.broadcasted_iota(jnp.int32, (step, 1), 0)
+        first = blocks[c // heads, 2 * i] * blk
+        second = (blocks[c // heads, 2 * i + 1] - 1) * blk
+        visible = pos_row[0:1, :] <= at + jnp.where(at < blk, first, second)
         s = jnp.where(visible, s, NEGATIVE)
         top = jnp.max(s, axis=1, keepdims=True)
         e = jnp.where(visible, jnp.exp(s - top), 0.0)
@@ -746,9 +776,9 @@
     lax.fori_loop(0, chips, attend, 0)
     back = from_owner(1, att_st, att, False)
     pass_w(4)
-    for m in (5, 6):
-        send_w(m, 0)
-        send_w(m, 1)
+    send_w(5, 0)
+    send_w(5, 1)
+    send_w(6, 0)
     own_gain2.wait()
     for copy in gain2:
         copy.wait_recv()
@@ -827,9 +857,11 @@
         along = [go(remote(mine, mine, zs.at[idx, i - 1], zr.at[idx, i - 1], ctx, zp(i))) for i in range(1, tps)]
         across = [go(remote(mine, mine, ps.at[idx, 0], pr.at[idx, 0], partner, z))]
 
-        def finish():
+        def finish(meanwhile=None):
             for i in range(1, tps):
                 along[i - 1].wait_recv()
+                if i == 2 and meanwhile is not None:
+                    meanwhile()
                 part = buf.at[ds(k * rows + ((z - i) % tps) * share_rows, share_rows), :]
                 across.append(go(remote(part, part, ps.at[idx, i], pr.at[idx, i], partner, z)))
             for copy in across:
@@ -855,10 +887,14 @@
     for copy in cot_z:
         copy.wait_recv()
     att_t[...] = jnp.transpose(att[...].reshape(both, head_w))
-    finish()
+
+    def more_weights():
+        pass_w(5)
+        send_w(6, 1)
+
+    finish(more_weights)
 
     fw = 256
-    pass_w(5)
     wait_w(4)
 
     def gate_step(j, carry):
@@ -869,7 +905,6 @@
     lax.fori_loop(0, ff_w // fw, gate_step, 0)
     for s in range(width // 256):
         hid_t[s * 256 : (s + 1) * 256, :] = jnp.transpose(hid[:, s * 256 : (s + 1) * 256])
-    pass_w(6)
     wait_w(5)
 
     def up_step(j, carry):
@@ -896,6 +931,8 @@
     def down_ready(i):
         if i == 0:
             w_own[6].wait()
+        if i == 1:
+            pass_w(6)
         got_w(6, *((4,), (0, 1), (2, 3), (5, 6))[i])
 
     value = reduce_rows(1, down_partial, from_chip, down_ready)
@@ -912,25 +949,59 @@
     gg_row[1:2, :] = jnp.sum(upstream * scaled, axis=0, keepdims=True)
     back_mix = m_inverse * gained - scaled * (m_inverse * m_inverse) * mean_of(gained * value)
     dmix[my_rows, :] = back_mix.astype(BF16)
-    spread(2, dmix)()
-
-    def dact_step(j, carry):
-        here = ds(j * fw, fw)
-        d_act = lax.dot_general(dmix[...], w[6][here, :], NT, preferred_element_type=F32)
-        dup[:, here] = (d_act * lin[:, here]).astype(BF16)
-        dgate[:, here] = (d_act * fac[:, here]).astype(BF16)
-        return carry
-
-    lax.fori_loop(0, ff_w // fw, dact_step, 0)
-
-    def gdown_step(j, carry):
-        here = ds(j * fw, fw)
-        w[6][:, here] = jnp.dot(act_t[...], dmix[:, here], preferred_element_type=F32).astype(BF16)
-        return carry
+    order = (far, near[0], near[1], c)
+
+    def mix_along(n, i):
+        here = dmix.at[my_rows, ds(order[n] * cw, cw)]
+        return remote(here, here, xs.at[n, i - 1], xr.at[n, i - 1], ctx, zp(i))
+
+    def mix_across(n, i):
+        owner = (z - i) % tps
+        here = dmix.at[ds(k * rows + owner * share_rows, share_rows), ds(order[n] * cw, cw)]
+        return remote(here, here, xs.at[n, tps - 1 + i], xr.at[n, tps - 1 + i], partner, z)
+
+    for n in range(chips):
+        for i in range(1, tps):
+            mix_along(n, i).start()
+        mix_across(n, 0).start()
 
     free_w(6)
-    lax.fori_loop(0, width // fw, gdown_step, 0)
-    send_g(6)
+    for n in range(chips):
+        for i in range(1, tps):
+            mix_along(n, i).wait_recv()
+            mix_across(n, i).start()
+        for i in range(tps):
+            mix_across(n, i).wait_recv()
+        off = order[n] * cw
+
+        def dact_step(j, carry):
+            here = ds(j * fw, fw)
+            d_act = lax.dot_general(dmix[:, ds(off, cw)], w[6][here, ds(off, cw)], NT, preferred_element_type=F32)
+            part = (ds((j // 2) * both, both), ds((j % 2) * fw, fw))
+            if n:
+                d_act = d_act + d_acc[part]
+            if n < chips - 1:
+                d_acc[part] = d_act
+            else:
+                dup[:, here] = (d_act * lin[:, here]).astype(BF16)
+                dgate[:, here] = (d_act * fac[:, here]).astype(BF16)
+            return carry
+
+        lax.fori_loop(0, ff_w // fw, dact_step, 0)
+        grad = jnp.dot(act_t[...], dmix[:, ds(off, cw)], preferred_element_type=F32)
+        w[6][:, ds(off, cw)] = grad.astype(BF16)
+        if n == 0:
+            send_far(6)
+        elif n < chips - 1:
+            send_near(6, n - 1)
+        else:
+            send_home(6)
+
+    for n in range(chips):
+        for i in range(1, tps):
+            mix_along(n, i).wait_send()
+        for i in range(tps):
+            mix_across(n, i).wait_send()
 
     def ff_partial(core, off):
         here = ds(core * rows, rows)
@@ -986,6 +1057,7 @@
     free_w(3)
     lax.fori_loop(0, width // fw, go_step, 0)
     arrive(pair)
+    dk_acc, dv_acc = d_acc.at[:, 0:HD], d_acc.at[:, HD : 2 * HD]
     dk_acc[...] = jnp.zeros((total, HD), F32)
     dv_acc[...] = jnp.zeros((total, HD), F32)
 
@@ -1145,19 +1217,12 @@
     heads = head_w // HD
     slab = width // (2 * chips)
     ctx = lax.axis_index("ctx")
-    chip = ctx // 2
-    pair = lax.dynamic_slice_in_dim(block_order, 2 * chip, 2, 1)
-    inner = jnp.arange(blk, dtype=jnp.int32)
-    positions = (pair.T[:, :, None] * blk + inner).reshape(both)
-    frequency = THETA ** (-2.0 * jnp.arange(HD // 2, dtype=F32) / HD)
-    angles = positions.astype(F32)[:, None] * frequency
-    cosine, sine = jnp.cos(angles), jnp.sin(angles)
-    cosf = jnp.concatenate([cosine, cosine], axis=1)
-    sinf = jnp.concatenate([-sine, sine], axis=1)
-    mine = lax.dynamic_slice_in_dim(block_order, chip // heads, 1, 0)
-    order = (mine.reshape(-1, 1) * blk + inner).reshape(total)
-    pos_row = jnp.broadcast_to(order[None, :], (8, total))
-    pos_col = jnp.broadcast_to(order[:, None], (total, 128))
+    frequency = THETA ** (-2.0 * np.arange(HD // 2) / HD)
+    frequency = np.concatenate([frequency, frequency])
+    starts = np.zeros((blk, 1))
+    starts[: 2 * chips, 0] = np.arange(2 * chips) * blk
+    inside = np.arange(blk)[:, None] * 1.0
+    table = np.stack([f(at * frequency) for at in (starts, inside) for f in (np.cos, np.sin)]).astype(np.float32)
     gains = jnp.stack([gain_query, gain_key, gain_attention, gain_feedforward]).astype(F32)
     gains = jnp.pad(gains, ((0, 4), (0, 0)))
     blank = jnp.zeros_like(gains)
@@ -1203,8 +1268,6 @@
         v((head_w, both)),
         v((2, seqs, blk, head_w)),
         v((2 * chips, blk, HD)),
-        v((total, HD), F32),
-        v((total, HD), F32),
         v((3, 2 * chips, blk, HD)),
         v((3, 2, seqs, blk, head_w)),
         v((2, 8, both), F32),
@@ -1243,6 +1306,12 @@
         dma((4, chips - 1)),
         dma((4, chips - 1)),
         dma((25,)),
+        v((2 * both, ff_w // 2), F32),
+        v((both, HD), F32),
+        v((both, HD), F32),
+        v((8, total), jnp.int32),
+        dma((chips, 2 * tps - 1)),
+        dma((chips, 2 * tps - 1)),
     ]
     results = pl.pallas_call(
         functools.partial(layer_kernel, dims),
@@ -1252,14 +1321,14 @@
             jax.ShapeDtypeStruct((8, 128), F32),
         ]
         + [jax.ShapeDtypeStruct((3,) + weight.shape, BF16) for weight in weights],
-        in_specs=[hbm] * 9 + [vmem] * 5,
+        in_specs=[hbm] * 9 + [pl.BlockSpec(memory_space=pltpu.SMEM), vmem, vmem],
         out_specs=[hbm, vmem, vmem] + [hbm] * 7,
         scratch_shapes=scratch,
         compiler_params=pltpu.CompilerParams(
             collective_id=0, has_side_effects=True, vmem_limit_bytes=67043328
         ),
         name="layer",
-    )(tokens.reshape(rows, feats), cotangent.reshape(rows, feats), *weights, gtile, cosf, sinf, pos_row, pos_col)
+    )(tokens.reshape(rows, feats), cotangent.reshape(rows, feats), *weights, block_order, gtile, table)
     output = results[0].reshape(tokens.shape)
     grad_input = results[1].reshape(tokens.shape)
     grads = [jnp.sum(received.astype(F32), axis=0) for received in results[3:]]

time: 396 us -> 384 us (0.970)
  Pallas kernels: 369 us -> 360 us
    pallas_call x1, Pallas kernels: 369 us -> 360 us  [fused(): pl.pallas_call(functools.partial(layer_kernel, dims), out_shape=[jax.Shap...]
    reduce_sum x7 -> x5, other arithmetic: 11.8 us -> 12.9 us  [fused(): grads = [jnp.sum(received.astype(F32), axis=0) for received in results[3:]]]
where the time goes in v3:
time: 384 us; the launch traced here: 379 us
  Pallas kernels  360 us (94%)
  other arithmetic  14.3 us (4%)
  local copies, waits for them, and re-layouts  3.92 us (1%)
    pallas_call x1, Pallas kernels, fused(): pl.pallas_call(functools.partial(layer_kernel, dims), out_shape=[jax.Shap...  360 us
    reduce_sum x5, other arithmetic, fused(): grads = [jnp.sum(received.astype(F32), axis=0) for received in results[3:]]  12.9 us

profile of v3, /device:TPU:0, one launch (start us, length us, event | category | flops | bytes accessed | tf_op | source)
XLA Modules:
  0.0 379.0 jit_solution(18118062446380790522)
XLA Ops:
  0.7 0.7 fusion.7
  1.4 0.7 pad_select_fusion.refs_10_
  2.0 360.1 %layer.1 = (f32[256,512]{1,0:T(8,128)}, f32[256,512]{1,0:T(8,128)}, f32[8,128]{1,0:T(8,128)}, bf16[3,256,512]{2,1,0:T(8,128)(2,1)}, bf16[3,256,512]{2,1,0:T(8,12...) custom-call(bf16[256,512]{1,0:T(8,128)(2,1)} %bitcast.18, ...), custom_call_target="tpu_custom_call" | custom-call | tf_op jit(solution)/shard_map/layer/pallas_call | solution.py:1316
  362.2 0.0 copy-start.2
  362.2 0.0 copy-start.3
  362.2 0.9 constant_dynamic-slice_fusion
  363.1 0.5 slice_bitcast_fusion
  363.6 2.1 convert_reduce_fusion.6
  365.7 0.0 copy-start
  365.7 2.2 convert_reduce_fusion.3
  367.9 0.0 copy-done.2
  367.9 0.0 copy-done.3
  367.9 1.2 convert_reduce_fusion.4
  369.1 0.0 copy-done
  369.1 0.0 copy-start.1
  369.1 1.7 convert_reduce_fusion
  370.9 0.9 copy-done.1
  371.8 0.0 copy-start.5
  371.8 0.0 copy-start.4
  371.8 5.6 %convert_reduce_fusion.1 = (f32[256,2048]{1,0:T(8,128)}, f32[256,2048]{1,0:T(8,128)}) fusion(bf16[3,256,2048]{2,1,0:T(8,128)(2,1)} %get-tuple-element.30, bf16[3,256,2048]{2,1,0:T(8,128)(2,1)S(1)} %copy-done.1), kind=kLoop, calls=%fused_computation.1 | loop fusion | flops 5242880 | bytes 10485760 | tf_op jit(solution)/shard_map/reduce_sum | solution.py:1334
  377.4 0.0 copy-done.5
  377.4 0.8 copy.30
  378.2 0.0 copy-done.4
  378.2 0.8 copy.31
Async XLA Ops:
  362.2 5.7 %copy-start.2 = (bf16[3,256,512]{2,1,0:T(8,128)(2,1)S(1)}, bf16[3,256,512]{2,1,0:T(8,128)(2,1)}, u32[]{:S(2)}) copy-start(bf16[3,256,512]{2,1,0:T(8,128)(2,1)} %get-tuple-element.26) | copy-start | bytes 2359300
  362.2 5.7 %copy-start.3 = (bf16[3,256,512]{2,1,0:T(8,128)(2,1)S(1)}, bf16[3,256,512]{2,1,0:T(8,128)(2,1)}, u32[]{:S(2)}) copy-start(bf16[3,256,512]{2,1,0:T(8,128)(2,1)} %get-tuple-element.27) | copy-start | bytes 2359300
  365.7 3.4 copy-start
  369.1 2.6 copy-start.1
  371.8 5.6 %copy-start.5 = (f32[256,512]{1,0:T(8,128)S(1)}, f32[256,512]{1,0:T(8,128)}, u32[]{:S(2)}) copy-start(f32[256,512]{1,0:T(8,128)} %get-tuple-element.23) | copy-start | bytes 1572868
  371.8 6.4 %copy-start.4 = (f32[256,512]{1,0:T(8,128)S(1)}, f32[256,512]{1,0:T(8,128)}, u32[]{:S(2)}) copy-start(f32[256,512]{1,0:T(8,128)} %get-tuple-element.24) | copy-start | bytes 1572868

commit v4 on v3

--- a/solution.py
+++ b/solution.py
@@ -437,6 +437,7 @@
     (blocks, gtile, table) = take(3)
     (out_ref, gin_ref, ggain_ref) = take(3)
     rx_g = take(7)
+    summed = take(4)
     w = take(7)
     via = take(7)
     (tok, tok_t, hid, hid_t, dmix, dattn) = take(6)
@@ -492,36 +493,38 @@
     for peer in peers:
         pl.semaphore_signal(barrier, inc=1, device_id=peer, device_id_type=MESH)
 
-    pending = []
-
     def go(copy):
         copy.start()
-        pending.append(copy)
         return copy
+
+    def sent(ref, sem):
+        remote(ref, ref, sem, sem, partner, z).wait_send()
+
+    def came(ref, sem):
+        remote(ref, ref, sem, sem, partner, z).wait_recv()
 
     def slab_of(m, owner):
         if m in COLS:
             return w[m].at[ds(owner * slab, slab), :]
         return w[m].at[:, ds(owner * slab, slab)]
 
+    def slabs(m, count):
+        return w[m].at[0 : count * slab, :] if m in COLS else w[m].at[:, 0 : count * slab]
+
     def half_of(m, core):
         if m in COLS:
             return w_in[m].at[:, ds(core * halves[m], halves[m])]
         return w_in[m].at[ds(core * halves[m], halves[m]), :]
 
     w_own = {}
-    w_pass = {}
     w_wait = {}
-
-    def w_slot(m, n, owner):
-        return remote(slab_of(m, owner), slab_of(m, owner), ws.at[m, n], wr.at[m, n], partner, z)
 
     def send_w(m, d):
         core = (k + d) % 2
         for n in range(2):
-            go(remote(half_of(m, core), slab_of(m, ctx), ws.at[m, 2 * n + d], wr.at[m, 2 * n + k], near[n] * 2 + core, z))
+            go(remote(half_of(m, core), slab_of(m, ctx), ws.at[m, 0], wr.at[m, 2 * n + k], near[n] * 2 + core, z))
         if d:
-            go(remote(half_of(m, ok), slab_of(m, ctx), ws.at[m, 4], wr.at[m, 4], partner, z))
+            go(remote(half_of(m, ok), slab_of(m, ctx), ws.at[m, 0], wr.at[m, 4], partner, z))
         else:
             w_own[m] = pltpu.make_async_copy(half_of(m, k), slab_of(m, ctx), loc.at[m])
             w_own[m].start()
@@ -535,19 +538,16 @@
         for n in which:
             if (m, n) not in w_wait:
                 w_wait[m, n] = True
-                w_slot(m, n, source(n)).wait_recv()
+                came(slabs(m, 1), wr.at[m, n])
 
     def pass_w(m):
         for n in range(2):
             got_w(m, 3 * n)
             mine = slab_of(m, source(3 * n))
-            copy = remote(mine, mine, ws.at[m, 5 + n], wr.at[m, 5 + n], near[1 - n] * 2 + k, z)
-            copy.start()
-            w_pass[m, n] = copy
+            go(remote(mine, mine, ws.at[m, 1], wr.at[m, 5 + n], near[1 - n] * 2 + k, z))
 
     def free_w(m):
-        for n in range(2):
-            w_pass[m, n].wait_send()
+        sent(slabs(m, 2), ws.at[m, 1])
 
     def wait_w(m):
         w_own[m].wait()
@@ -558,21 +558,20 @@
             return rx_g[m].at[n, :, ds(core * halves[m], halves[m])]
         return rx_g[m].at[n, ds(core * halves[m], halves[m]), :]
 
-    g_live = []
-    g_own = []
+    g_own = {}
 
     def send_far(m):
         for n in range(2):
-            go(remote(slab_of(m, far * 2 + n), via[m].at[n], gs.at[m, n], gr.at[m, n], near[n] * 2 + k, z))
+            go(remote(slab_of(m, far * 2 + n), via[m].at[n], gs.at[m], gr.at[m, n], near[n] * 2 + k, z))
 
     def send_near(m, n):
-        go(remote(slab_of(m, near[n] * 2 + n), into(m, 1 + n, k), gs.at[m, 2 + n], gr.at[m, 2 + 2 * n + k], near[n] * 2 + n, z))
+        go(remote(slab_of(m, near[n] * 2 + n), into(m, 1 + n, k), gs.at[m], gr.at[m, 2], near[n] * 2 + n, z))
 
     def send_home(m):
-        go(remote(slab_of(m, partner), into(m, 0, k), gs.at[m, 6], gr.at[m, 6], partner, z))
+        go(remote(slab_of(m, partner), into(m, 0, k), gs.at[m], gr.at[m, 2], partner, z))
         copy = pltpu.make_async_copy(slab_of(m, ctx), into(m, 0, k), loc.at[8 + m])
         copy.start()
-        g_own.append(copy)
+        g_own[m] = copy
 
     def send_g(m):
         send_far(m)
@@ -583,19 +582,39 @@
     def pass_g(m):
         for n in range(2):
             to = near[1 - n] * 2 + n
-            remote(via[m].at[n], via[m].at[n], gs.at[m, n], gr.at[m, n], partner, z).wait_recv()
+            came(via[m].at[n], gr.at[m, n])
             total = slab_of(m, to)[...].astype(F32) + via[m][n].astype(F32)
             slab_of(m, to)[...] = total.astype(BF16)
-            go(remote(slab_of(m, to), into(m, 2 - n, k), gs.at[m, 4 + n], gr.at[m, 2 + 2 * (1 - n) + k], to, z))
-        g_live.append(m)
+            go(remote(slab_of(m, to), into(m, 2 - n, k), gs.at[m], gr.at[m, 2], to, z))
 
     def wait_g(m):
-        for n in range(2):
-            for core in range(2):
-                here = into(m, 1 + n, core)
-                remote(here, here, gs.at[m, 0], gr.at[m, 2 + 2 * n + core], partner, z).wait_recv()
-        here = into(m, 0, ok)
-        remote(here, here, gs.at[m, 6], gr.at[m, 6], partner, z).wait_recv()
+        g_own[m].wait()
+        came(slabs(m, 5), gr.at[m, 2])
+
+    def add_up(m):
+        wait_g(m)
+        if m in COLS:
+            n = slab
+            parts = (hid.at[0:n, :], hid.at[n : 2 * n, :], dmix.at[0:n, :], dmix.at[n : 2 * n, :])
+        else:
+            n = 2 * halves[m]
+            parts = (hid_t.at[0:n, 0:slab], hid_t.at[0:n, slab : 2 * slab], tok_t.at[0:n, 0:slab], tok_t.at[0:n, slab : 2 * slab])
+        loads = [pltpu.make_async_copy(rx_g[m].at[i], parts[i], loc.at[i]) for i in range(3)]
+        for copy in loads:
+            copy.start()
+        for copy in loads:
+            copy.wait()
+
+        def add_step(j, carry):
+            here = (slice(None), ds(j * 256, 256)) if m in COLS else (ds(j * 256, 256), slice(None))
+            value = parts[0][here].astype(F32) + parts[1][here].astype(F32) + parts[2][here].astype(F32)
+            parts[3][here] = value.astype(BF16)
+            return carry
+
+        lax.fori_loop(0, 2 * halves[m] // 256, add_step, 0)
+        copy = pltpu.make_async_copy(parts[3], summed[m - 3], loc.at[3])
+        copy.start()
+        copy.wait()
 
     own_tok = pltpu.make_async_copy(tok_in, tok.at[ds(k * rows, rows), ds(z * feats, feats)], loc.at[16])
     own_tok.start()
@@ -605,32 +624,25 @@
     own_gain.start()
     pl.semaphore_wait(barrier, len(peers))
 
-    tok_z = []
     for i in range(1, tps):
-        tok_z.append(go(remote(tok_in, tok.at[ds(k * rows, rows), ds(z * feats, feats)], zs.at[0, i - 1], zr.at[0, i - 1], ctx, zp(i))))
-    tok_p = [go(remote(tok_in, tok.at[ds(k * rows, rows), ds(z * feats, feats)], ps.at[0, 0], pr.at[0, 0], partner, z))]
+        go(remote(tok_in, tok.at[ds(k * rows, rows), ds(z * feats, feats)], zs.at[0], zr.at[0, i - 1], ctx, zp(i)))
+    go(remote(tok_in, tok.at[ds(k * rows, rows), ds(z * feats, feats)], ps.at[0], pr.at[0], partner, z))
     slots = [(i, d) for i in range(chips) for d in range(2)]
-    gain1 = []
-    n = 0
     for i, d in slots:
         if i or d:
-            gain1.append(go(remote(gtile, gbuf.at[ctx], ms.at[0, n], mr.at[0, n], chip(i) * 2 + (k + d) % 2, z)))
-            n += 1
-    cot_z = []
+            go(remote(gtile, gbuf.at[ctx], ms.at[0], mr.at[0], chip(i) * 2 + (k + d) % 2, z))
     for i in range(1, tps):
-        cot_z.append(go(remote(cot_in.at[ds(zp(i) * share_rows, share_rows), :], cot.at[:, ds(z * feats, feats)], ms.at[1, i - 1], mr.at[1, i - 1], ctx, zp(i))))
+        go(remote(cot_in.at[ds(zp(i) * share_rows, share_rows), :], cot.at[:, ds(z * feats, feats)], ms.at[1], mr.at[1], ctx, zp(i)))
     for m in (0, 1, 2, 3):
         send_w(m, 0)
         send_w(m, 1)
 
     own_gain.wait()
-    for copy in gain1:
-        copy.wait_recv()
+    came(gbuf.at[0 : 2 * chips - 1], mr.at[0])
     own_gain2 = pltpu.make_async_copy(gbuf, gall.at[z], loc.at[19])
     own_gain2.start()
-    gain2 = []
     for i in range(1, tps):
-        gain2.append(go(remote(gbuf, gall.at[z], ms.at[2, i - 1], mr.at[2, i - 1], ctx, zp(i))))
+        go(remote(gbuf, gall.at[z], ms.at[2], mr.at[2], ctx, zp(i)))
     for r in range(2):
         pieces = [gbuf[4 * k + 2 * m, r : r + 1, :] + gbuf[4 * k + 2 * m + 1, r : r + 1, :] for m in range(head_w // 128)]
         gqk[r : r + 1, :] = jnp.concatenate(pieces, axis=1)
@@ -652,14 +664,13 @@
 
     own_tok.wait()
     for i in range(1, tps):
-        tok_z[i - 1].wait_recv()
+        came(tok.at[0:rows, 0:feats], zr.at[0, i - 1])
         part = tok.at[ds(k * rows, rows), ds(((z - i) % tps) * feats, feats)]
-        tok_p.append(go(remote(part, part, ps.at[0, i], pr.at[0, i], partner, z)))
+        go(remote(part, part, ps.at[0], pr.at[0], partner, z))
     for m in (0, 1, 2, 3):
         pass_w(m)
     send_w(4, 0)
-    for copy in tok_p:
-        copy.wait_recv()
+    came(tok.at[0:rows, :], pr.at[0])
 
     def row_of(value):
         folded = value[:, :128]
@@ -671,17 +682,16 @@
         return jnp.transpose(jnp.broadcast_to(row, (128, both)))
 
     def totals(idx):
-        copies = []
         n = 0
         for i in range(tps):
             for d in range(2):
                 if i or d:
                     to = ctx if d == 0 else partner
-                    copies.append(go(remote(sq_own.at[idx], sq_rx.at[idx, n], ss.at[idx, n], sr.at[idx, n], to, zp(i))))
+                    go(remote(sq_own.at[idx], sq_rx.at[idx, n], ss.at[idx], sr.at[idx], to, zp(i)))
                     n += 1
+        came(sq_rx.at[idx], sr.at[idx])
         total = sq_own[idx]
-        for j, copy in enumerate(copies):
-            copy.wait_recv()
+        for j in range(n):
             total = total + sq_rx[idx, j]
         return total
 
@@ -709,7 +719,7 @@
             qkv[t, :, :, :, lanes] = turned.astype(BF16).reshape(2, seqs, blk, HD)
 
     def to_owner(idx, value, owned, stacked):
-        copies = []
+        size = owned.at[:, 0 : 2 * chips - 2] if stacked else owned.at[0 : 2 * chips - 2]
         for i in range(chips):
             to = chip(i)
             s, h = to // heads, to % heads
@@ -720,15 +730,15 @@
                 src = value.at[:, s, :, ds(h * HD, HD)]
                 dst = owned.at[ds(2 * c, 2)]
             if i:
-                copies.append(go(remote(src, dst, as_.at[idx, i - 1], ar.at[idx, i - 1], to * 2 + k, z)))
+                go(remote(src, dst, as_.at[idx], ar.at[idx], to * 2 + k, z))
             else:
                 own = pltpu.make_async_copy(src, dst, loc.at[20 + idx])
                 own.start()
-        return own, copies
+        return own, size, idx
 
     def from_owner(idx, owned, value, stacked):
+        size = owned.at[:, 0 : 2 * chips - 2] if stacked else owned.at[0 : 2 * chips - 2]
         s, h = c // heads, c % heads
-        copies = []
         for i in range(chips):
             to = chip(i)
             if stacked:
@@ -738,17 +748,17 @@
                 src = owned.at[ds(2 * to, 2)]
                 dst = value.at[:, s, :, ds(h * HD, HD)]
             if i:
-                copies.append(go(remote(src, dst, as_.at[idx, i - 1], ar.at[idx, i - 1], to * 2 + k, z)))
+                go(remote(src, dst, as_.at[idx], ar.at[idx], to * 2 + k, z))
             else:
                 own = pltpu.make_async_copy(src, dst, loc.at[20 + idx])
                 own.start()
-        return own, copies
+        return own, size, idx
 
     def arrive(pair):
-        own, copies = pair
+        own, size, idx = pair
         own.wait()
-        for copy in copies:
-            copy.wait_recv()
+        came(size, ar.at[idx])
+        sent(size, as_.at[idx])
 
     pair = to_owner(0, qkv, qa, True)
     send_w(4, 1)
@@ -780,8 +790,7 @@
     send_w(5, 1)
     send_w(6, 0)
     own_gain2.wait()
-    for copy in gain2:
-        copy.wait_recv()
+    came(gall.at[0 : tps - 1], mr.at[2])
     for r in range(2):
         pieces = []
         for zz in range(tps):
@@ -797,14 +806,14 @@
     rs_live = {}
 
     def rp_copy(idx, i, off):
-        return remote(st_p.at[:, ds(off, cw)], rx_p.at[idx % 2, :, ds(off, cw)], rps.at[idx, i], rpr.at[idx, i], partner, z)
+        return remote(st_p.at[:, ds(off, cw)], rx_p.at[idx % 2, :, ds(off, cw)], rps.at[idx], rpr.at[idx, i], partner, z)
 
     def rz_copy(idx, i, j, off):
         return remote(
             st_z.at[ds(zp(j) * share_rows, share_rows), ds(off, cw)],
             rx_z.at[idx % 2, j - 1, :, ds(off, cw)],
-            rzs.at[idx, i, j - 1],
-            rzr.at[idx, i, j - 1],
+            rzs.at[idx],
+            rzr.at[idx],
             ctx,
             zp(j),
         )
@@ -822,13 +831,6 @@
             for j in range(1, tps):
                 rz_copy(idx, i, j, off).start()
 
-        def finish(i):
-            off = offset(i)
-            for j in range(1, tps):
-                rz_copy(idx, i, j, off).wait_recv()
-                rz_copy(idx, i, j, off).wait_send()
-            rp_copy(idx, i, off).wait_send()
-
         if before is None:
             lax.fori_loop(0, tps, lambda i, x: (one(i), x)[1], 0)
         else:
@@ -836,11 +838,9 @@
                 one(i)
         if meanwhile is not None:
             meanwhile()
-        if before is None:
-            lax.fori_loop(0, tps, lambda i, x: (finish(i), x)[1], 0)
-        else:
-            for i in range(tps):
-                finish(i)
+        came(rx_z.at[idx % 2], rzr.at[idx])
+        sent(rx_z.at[idx % 2], rzs.at[idx])
+        sent(st_p, rps.at[idx])
         mine = st_z[ds(z * share_rows, share_rows), :].astype(F32)
         for j in range(tps - 1):
             mine = mine + rx_z[idx % 2, j].astype(F32)
@@ -854,18 +854,20 @@
 
     def spread(idx, buf):
         mine = buf.at[ds(k * rows + z * share_rows, share_rows), :]
-        along = [go(remote(mine, mine, zs.at[idx, i - 1], zr.at[idx, i - 1], ctx, zp(i))) for i in range(1, tps)]
-        across = [go(remote(mine, mine, ps.at[idx, 0], pr.at[idx, 0], partner, z))]
+        for i in range(1, tps):
+            go(remote(mine, mine, zs.at[idx], zr.at[idx, i - 1], ctx, zp(i)))
+        go(remote(mine, mine, ps.at[idx], pr.at[idx], partner, z))
 
         def finish(meanwhile=None):
             for i in range(1, tps):
-                along[i - 1].wait_recv()
+                came(buf.at[0:share_rows, :], zr.at[idx, i - 1])
                 if i == 2 and meanwhile is not None:
                     meanwhile()
                 part = buf.at[ds(k * rows + ((z - i) % tps) * share_rows, share_rows), :]
-                across.append(go(remote(part, part, ps.at[idx, i], pr.at[idx, i], partner, z)))
-            for copy in across:
-                copy.wait_recv()
+                go(remote(part, part, ps.at[idx], pr.at[idx], partner, z))
+            came(buf.at[0:rows, :], pr.at[idx])
+            sent(buf.at[0 : (tps - 1) * share_rows, :], zs.at[idx])
+            sent(buf.at[0:rows, :], ps.at[idx])
 
         return finish
 
@@ -884,8 +886,7 @@
     hid[my_rows, :] = state.astype(BF16)
     finish = spread(1, hid)
     own_cot.wait()
-    for copy in cot_z:
-        copy.wait_recv()
+    came(cot.at[:, 0 : (tps - 1) * feats], mr.at[1])
     att_t[...] = jnp.transpose(att[...].reshape(both, head_w))
 
     def more_weights():
@@ -938,40 +939,39 @@
     value = reduce_rows(1, down_partial, from_chip, down_ready)
     m_inverse = lax.rsqrt(mean_of(value * value) + EPS)
     scaled = value * m_inverse
-    stage[...] = hstate[...] + scaled * gfull[1:2, :]
-    for i in range(1, tps):
-        go(remote(stage.at[:, ds(zp(i) * feats, feats)], out_ref.at[ds(z * share_rows, share_rows), :], ms.at[3, i - 1], mr.at[3, i - 1], ctx, zp(i)))
-    out_z = pending[-(tps - 1) :]
-    own_out = pltpu.make_async_copy(stage.at[:, ds(z * feats, feats)], out_ref.at[ds(z * share_rows, share_rows), :], loc.at[24])
-    own_out.start()
     upstream = cot[...].astype(F32)
     gained = upstream * gfull[1:2, :]
-    gg_row[1:2, :] = jnp.sum(upstream * scaled, axis=0, keepdims=True)
     back_mix = m_inverse * gained - scaled * (m_inverse * m_inverse) * mean_of(gained * value)
     dmix[my_rows, :] = back_mix.astype(BF16)
     order = (far, near[0], near[1], c)
 
     def mix_along(n, i):
         here = dmix.at[my_rows, ds(order[n] * cw, cw)]
-        return remote(here, here, xs.at[n, i - 1], xr.at[n, i - 1], ctx, zp(i))
+        return remote(here, here, xs.at[n], xr.at[n], ctx, zp(i))
 
     def mix_across(n, i):
         owner = (z - i) % tps
         here = dmix.at[ds(k * rows + owner * share_rows, share_rows), ds(order[n] * cw, cw)]
-        return remote(here, here, xs.at[n, tps - 1 + i], xr.at[n, tps - 1 + i], partner, z)
-
-    for n in range(chips):
+        return remote(here, here, xs.at[chips], xr.at[chips + n], partner, z)
+
+    def mix_start(n):
         for i in range(1, tps):
             mix_along(n, i).start()
         mix_across(n, 0).start()
 
+    mix_start(0)
+    gg_row[1:2, :] = jnp.sum(upstream * scaled, axis=0, keepdims=True)
+    stage[...] = hstate[...] + scaled * gfull[1:2, :]
+
     free_w(6)
     for n in range(chips):
+        sent(dmix.at[0:share_rows, 0 : (tps - 1) * cw], xs.at[n])
+        if n < chips - 1:
+            mix_start(n + 1)
+        came(dmix.at[0:share_rows, 0 : (tps - 1) * cw], xr.at[n])
         for i in range(1, tps):
-            mix_along(n, i).wait_recv()
             mix_across(n, i).start()
-        for i in range(tps):
-            mix_across(n, i).wait_recv()
+        came(dmix.at[0:rows, 0:cw], xr.at[chips + n])
         off = order[n] * cw
 
         def dact_step(j, carry):
@@ -997,11 +997,11 @@
         else:
             send_home(6)
 
-    for n in range(chips):
-        for i in range(1, tps):
-            mix_along(n, i).wait_send()
-        for i in range(tps):
-            mix_across(n, i).wait_send()
+    sent(dmix.at[0:rows, :], xs.at[chips])
+    for i in range(1, tps):
+        go(remote(stage.at[:, ds(zp(i) * feats, feats)], out_ref.at[ds(z * share_rows, share_rows), :], ms.at[3], mr.at[3], ctx, zp(i)))
+    own_out = pltpu.make_async_copy(stage.at[:, ds(z * feats, feats)], out_ref.at[ds(z * share_rows, share_rows), :], loc.at[24])
+    own_out.start()
 
     def ff_partial(core, off):
         here = ds(core * rows, rows)
@@ -1031,9 +1031,8 @@
     back_att = a_inverse * gained - scaled * (a_inverse * a_inverse) * mean_of(gained * projected)
     dattn[my_rows, :] = back_att.astype(BF16)
     finish = spread(3, dattn)
-    gains_z = []
     for i in range(1, tps):
-        gains_z.append(go(remote(gg_row.at[:, ds(zp(i) * feats, feats)], gg_rx1.at[i - 1], ms.at[4, i - 1], mr.at[4, i - 1], ctx, zp(i))))
+        go(remote(gg_row.at[:, ds(zp(i) * feats, feats)], gg_rx1.at[i - 1], ms.at[4], mr.at[4], ctx, zp(i)))
 
     def gup_step(j, carry):
         here = ds(j * fw, fw)
@@ -1111,7 +1110,7 @@
             dqkv[t, :, :, :, lanes] = grad.astype(BF16).reshape(2, seqs, blk, HD)
 
     def rf_copy(i, off):
-        return remote(st_z.at[:, ds(off, cw)], rx_f.at[i], rzs.at[3, i, 0], rzr.at[3, i, 0], ctx, zp(i + 1))
+        return remote(st_z.at[:, ds(off, cw)], rx_f.at[i], rzs.at[3], rzr.at[3], ctx, zp(i + 1))
 
     def in_partial(core, off):
         here = ds(off, cw)
@@ -1148,44 +1147,52 @@
         lax.fori_loop(0, width // 512, gqkv_step, 0)
         send_g(m)
     middle = gg_row[:, ds(z * feats, feats)]
-    for i, copy in enumerate(gains_z):
-        copy.wait_recv()
+    came(gg_rx1, mr.at[4])
+    for i in range(tps - 1):
         middle = middle + gg_rx1[i]
     gg_mid[...] = gg_mid[...] + middle
-    gains_c = []
     n = 0
     for i, d in slots:
         if i or d:
             core = (k + d) % 2
-            gains_c.append(go(remote(gg_mid.at[:, ds(chip(i) * 128, 128)], gg_rx2.at[n], ms.at[5, n], mr.at[5, n], chip(i) * 2 + core, z)))
+            go(remote(gg_mid.at[:, ds(chip(i) * 128, 128)], gg_rx2.at[n], ms.at[5], mr.at[5], chip(i) * 2 + core, z))
             n += 1
 
+    add_up(6)
+    add_up(4)
     for m in range(3):
         pass_g(m)
-    for i in range(tps - 1):
-        rf_copy(i, zp(i + 1) * cw).wait_recv()
+    add_up(3)
+    add_up(5)
+    came(rx_f, rzr.at[3])
+    sent(rx_f, rzs.at[3])
+    sent(st_p, rps.at[3])
     final = st_z[:, ds(z * feats, cw)].astype(F32)
     for i in range(tps - 1):
         final = final + rx_f[i].astype(F32)
     gin_ref[...] = final
-    for i in range(tps):
-        rp_copy(3, i, zp(i + 1) * cw).wait_send()
-        if i < tps - 1:
-            rf_copy(i, zp(i + 1) * cw).wait_send()
     gain_sum = gg_mid[:, ds(c * 128, 128)]
-    for i, copy in enumerate(gains_c):
-        copy.wait_recv()
+    came(gg_rx2, mr.at[5])
+    for i in range(2 * chips - 1):
         gain_sum = gain_sum + gg_rx2[i]
-    ggain_ref[...] = gain_sum
+    ggain_ref[...] = jnp.where(k == 1, pltpu.roll(gain_sum, 64, 1), gain_sum)
     own_out.wait()
-    for copy in out_z:
-        copy.wait_recv()
-    for copy in g_own:
-        copy.wait()
-    for m in g_live:
+    came(stage.at[:, 0 : (tps - 1) * feats], mr.at[3])
+    for m in range(3):
         wait_g(m)
-    for copy in pending:
-        copy.wait_send()
+    sent(tok.at[0:rows, 0 : (tps - 1) * feats], zs.at[0])
+    sent(tok.at[0:rows, :], ps.at[0])
+    sent(gbuf.at[0 : 2 * chips - 1], ms.at[0])
+    sent(cot.at[:, 0 : (tps - 1) * feats], ms.at[1])
+    sent(gall.at[0 : tps - 1], ms.at[2])
+    sent(stage.at[:, 0 : (tps - 1) * feats], ms.at[3])
+    sent(gg_rx1, ms.at[4])
+    sent(gg_rx2, ms.at[5])
+    for idx in range(2):
+        sent(sq_rx.at[idx], ss.at[idx])
+    for m in range(7):
+        sent(slabs(m, 5), ws.at[m, 0])
+        sent(slabs(m, 7), gs.at[m])
 
 
 def fused(
@@ -1287,31 +1294,31 @@
         v((tps - 1, 8, feats), F32),
         v((8, feats), F32),
         v((2 * chips - 1, 8, 128), F32),
-        dma((7, 2 * chips)),
-        dma((7, 2 * chips)),
-        dma((7, 2 * chips)),
-        dma((7, 2 * chips)),
+        dma((7, 2)),
+        dma((7, 7)),
+        dma((7,)),
+        dma((7, 3)),
+        dma((4,)),
         dma((4, tps - 1)),
-        dma((4, tps - 1)),
+        dma((4,)),
+        dma((4,)),
+        dma((4,)),
         dma((4, tps)),
-        dma((4, tps)),
-        dma((4, tps)),
-        dma((4, tps)),
-        dma((4, tps, tps - 1)),
-        dma((4, tps, tps - 1)),
-        dma((6, 2 * chips)),
-        dma((6, 2 * chips)),
-        dma((2, 2 * tps - 1)),
-        dma((2, 2 * tps - 1)),
-        dma((4, chips - 1)),
-        dma((4, chips - 1)),
+        dma((4,)),
+        dma((4,)),
+        dma((6,)),
+        dma((6,)),
+        dma((2,)),
+        dma((2,)),
+        dma((4,)),
+        dma((4,)),
         dma((25,)),
         v((2 * both, ff_w // 2), F32),
         v((both, HD), F32),
         v((both, HD), F32),
         v((8, total), jnp.int32),
-        dma((chips, 2 * tps - 1)),
-        dma((chips, 2 * tps - 1)),
+        dma((chips + 1,)),
+        dma((2 * chips,)),
     ]
     results = pl.pallas_call(
         functools.partial(layer_kernel, dims),
@@ -1320,9 +1327,10 @@
             jax.ShapeDtypeStruct((rows, feats), F32),
             jax.ShapeDtypeStruct((8, 128), F32),
         ]
-        + [jax.ShapeDtypeStruct((3,) + weight.shape, BF16) for weight in weights],
+        + [jax.ShapeDtypeStruct((3,) + weight.shape, BF16) for weight in weights]
+        + [jax.ShapeDtypeStruct(weight.shape, BF16) for weight in weights[3:]],
         in_specs=[hbm] * 9 + [pl.BlockSpec(memory_space=pltpu.SMEM), vmem, vmem],
-        out_specs=[hbm, vmem, vmem] + [hbm] * 7,
+        out_specs=[hbm, vmem, vmem] + [hbm] * 11,
         scratch_shapes=scratch,
         compiler_params=pltpu.CompilerParams(
             collective_id=0, has_side_effects=True, vmem_limit_bytes=67043328
@@ -1331,8 +1339,9 @@
     )(tokens.reshape(rows, feats), cotangent.reshape(rows, feats), *weights, block_order, gtile, table)
     output = results[0].reshape(tokens.shape)
     grad_input = results[1].reshape(tokens.shape)
-    grads = [jnp.sum(received.astype(F32), axis=0) for received in results[3:]]
-    lanes = lax.dynamic_slice_in_dim(results[2], (ctx % 2) * 64, 64, 1)
+    grads = [jnp.sum(received.astype(F32), axis=0) for received in results[3:6]]
+    grads += [value.astype(F32) for value in results[10:]]
+    lanes = results[2][:, :64]
     return (output, grad_input, *grads, lanes[2], lanes[3], lanes[0], lanes[1])
 
 

time: 384 us -> 374 us (0.974)
  Pallas kernels: 360 us -> 354 us
    reduce_sum x5 -> x2, other arithmetic: 12.9 us -> 3.37 us  [fused(): grads = [jnp.sum(received.astype(F32), axis=0) for received in results[3:6]]]
    convert_element_type x0 -> x4, other arithmetic: none -> 6.37 us  [fused(): grads += [value.astype(F32) for value in results[10:]]]
    pallas_call x1, Pallas kernels: 360 us -> 354 us  [fused(): pl.pallas_call(functools.partial(layer_kernel, dims), out_shape=[jax.Shap...]
where the time goes in v4:
time: 374 us; the launch traced here: 369 us
  Pallas kernels  354 us (95%)
  other arithmetic  11.1 us (3%)
    pallas_call x1, Pallas kernels, fused(): pl.pallas_call(functools.partial(layer_kernel, dims), out_shape=[jax.Shap...  354 us

profile of v4, /device:TPU:0, one launch (start us, length us, event | category | flops | bytes accessed | tf_op | source)
XLA Modules:
  0.0 368.9 jit_solution(960424706678874133)
XLA Ops:
  0.7 0.7 fusion.7
  1.4 0.7 pad_select_fusion.refs_10_
  2.0 354.1 %layer.1 = (f32[256,512]{1,0:T(8,128)}, f32[256,512]{1,0:T(8,128)}, f32[8,128]{1,0:T(8,128)}, bf16[3,256,512]{2,1,0:T(8,128)(2,1)}, bf16[3,256,512]{2,1,0:T(8,12...) custom-call(bf16[256,512]{1,0:T(8,128)(2,1)} %bitcast.18, ...), custom_call_target="tpu_custom_call" | custom-call | tf_op jit(solution)/shard_map/layer/pallas_call | solution.py:1323
  356.2 0.0 copy-start.3
  356.2 0.0 copy-start.4
  356.2 1.3 slice_bitcast_fusion
  357.6 0.0 copy-start.2
  357.6 2.2 convert_reduce_fusion.2
  359.7 1.8 convert_element_type.27
  361.5 0.0 copy-done.3
  361.5 0.0 copy-done.4
  361.5 1.2 convert_reduce_fusion
  362.7 0.0 copy-start.1
  362.7 0.0 copy-done.2
  362.7 1.6 convert_element_type.28
  364.3 0.0 copy-done.1
  364.3 0.0 copy-start
  364.3 1.6 convert_element_type.29
  365.8 0.0 copy-done
  365.8 0.0 copy-start.6
  365.8 0.0 copy-start.5
  365.8 1.5 convert_element_type.30
  367.3 0.0 copy-done.6
  367.3 0.8 copy.30
  368.1 0.0 copy-done.5
  368.1 0.8 copy.31
Async XLA Ops:
  356.2 5.3 %copy-start.3 = (bf16[3,256,512]{2,1,0:T(8,128)(2,1)S(1)}, bf16[3,256,512]{2,1,0:T(8,128)(2,1)}, u32[]{:S(2)}) copy-start(bf16[3,256,512]{2,1,0:T(8,128)(2,1)} %get-tuple-element.26) | copy-start | bytes 2359300
  356.2 5.3 %copy-start.4 = (bf16[3,256,512]{2,1,0:T(8,128)(2,1)S(1)}, bf16[3,256,512]{2,1,0:T(8,128)(2,1)}, u32[]{:S(2)}) copy-start(bf16[3,256,512]{2,1,0:T(8,128)(2,1)} %get-tuple-element.27) | copy-start | bytes 2359300
  357.6 5.2 %copy-start.2 = (bf16[256,2048]{1,0:T(8,128)(2,1)S(1)}, bf16[256,2048]{1,0:T(8,128)(2,1)}, u32[]{:S(2)}) copy-start(bf16[256,2048]{1,0:T(8,128)(2,1)} %get-tuple-element.29) | copy-start | bytes 3145732
  362.7 1.6 copy-start.1
  364.3 1.6 copy-start
  365.8 1.5 copy-start.6
  365.8 2.3 copy-start.5

commit v5 on v4

--- a/solution.py
+++ b/solution.py
@@ -434,7 +434,7 @@
 
     (tok_in, cot_in) = take(2)
     w_in = take(7)
-    (blocks, gtile, table) = take(3)
+    (blocks, *gains, table) = take(6)
     (out_ref, gin_ref, ggain_ref) = take(3)
     rx_g = take(7)
     summed = take(4)
@@ -455,7 +455,7 @@
     (ss, sr) = take(2)
     (as_, ar) = take(2)
     (loc,) = take(1)
-    (d_acc, cosf, sinf, pos_row) = take(4)
+    (d_acc, cosf, sinf, pos_row, gtile) = take(5)
     (xs, xr) = take(2)
 
     ctx = lax.axis_index("ctx")
@@ -616,13 +616,19 @@
         copy.start()
         copy.wait()
 
+    lane = lax.broadcasted_iota(jnp.int32, (blk, HD), 1)
+    gtile[...] = jnp.zeros((8, 128), F32)
+    for r in range(4):
+        value = gains[r][...].astype(F32)
+        value = jnp.concatenate([value, value], axis=1)
+        gtile[r : r + 1, :] = jnp.where(lane[0:1, :] // 64 == k, value, 0.0)
     own_tok = pltpu.make_async_copy(tok_in, tok.at[ds(k * rows, rows), ds(z * feats, feats)], loc.at[16])
     own_tok.start()
     own_cot = pltpu.make_async_copy(cot_in.at[ds(z * share_rows, share_rows), :], cot.at[:, ds(z * feats, feats)], loc.at[17])
     own_cot.start()
+    pl.semaphore_wait(barrier, len(peers))
     own_gain = pltpu.make_async_copy(gtile, gbuf.at[ctx], loc.at[18])
     own_gain.start()
-    pl.semaphore_wait(barrier, len(peers))
 
     for i in range(1, tps):
         go(remote(tok_in, tok.at[ds(k * rows, rows), ds(z * feats, feats)], zs.at[0], zr.at[0, i - 1], ctx, zp(i)))
@@ -647,7 +653,6 @@
         pieces = [gbuf[4 * k + 2 * m, r : r + 1, :] + gbuf[4 * k + 2 * m + 1, r : r + 1, :] for m in range(head_w // 128)]
         gqk[r : r + 1, :] = jnp.concatenate(pieces, axis=1)
 
-    lane = lax.broadcasted_iota(jnp.int32, (blk, HD), 1)
     sign = jnp.where(lane < HD // 2, -1.0, 1.0)
     for core in range(2):
         for s in range(seqs):
@@ -663,13 +668,14 @@
         pos_row[:, here] = start + lane[0:8, :]
 
     own_tok.wait()
+    pass_w(0)
     for i in range(1, tps):
+        pass_w(i)
+        if i == tps - 1:
+            send_w(4, 0)
         came(tok.at[0:rows, 0:feats], zr.at[0, i - 1])
         part = tok.at[ds(k * rows, rows), ds(((z - i) % tps) * feats, feats)]
         go(remote(part, part, ps.at[0], pr.at[0], partner, z))
-    for m in (0, 1, 2, 3):
-        pass_w(m)
-    send_w(4, 0)
     came(tok.at[0:rows, :], pr.at[0])
 
     def row_of(value):
@@ -861,7 +867,7 @@
         def finish(meanwhile=None):
             for i in range(1, tps):
                 came(buf.at[0:share_rows, :], zr.at[idx, i - 1])
-                if i == 2 and meanwhile is not None:
+                if i == 1 and meanwhile is not None:
                     meanwhile()
                 part = buf.at[ds(k * rows + ((z - i) % tps) * share_rows, share_rows), :]
                 go(remote(part, part, ps.at[idx], pr.at[idx], partner, z))
@@ -932,7 +938,6 @@
     def down_ready(i):
         if i == 0:
             w_own[6].wait()
-        if i == 1:
             pass_w(6)
         got_w(6, *((4,), (0, 1), (2, 3), (5, 6))[i])
 
@@ -1014,12 +1019,20 @@
         w[4][:, here] = jnp.dot(hid_t[...], dgate[:, here], preferred_element_type=F32).astype(BF16)
         return carry
 
+    def gup_step(j, carry):
+        here = ds(j * fw, fw)
+        w[5][:, here] = jnp.dot(hid_t[...], dup[:, here], preferred_element_type=F32).astype(BF16)
+        return carry
+
     def gate_grad():
         free_w(4)
         lax.fori_loop(0, ff_w // fw, ggate_step, 0)
-        pass_g(6)
         send_g(4)
-
+        free_w(5)
+        lax.fori_loop(0, ff_w // fw, gup_step, 0)
+        send_far(5)
+
+    pass_g(6)
     value = reduce_rows(2, ff_partial, straight, meanwhile=gate_grad) + cot[...].astype(F32)
     dhid[...] = value
     projected = proj[...]
@@ -1034,19 +1047,14 @@
     for i in range(1, tps):
         go(remote(gg_row.at[:, ds(zp(i) * feats, feats)], gg_rx1.at[i - 1], ms.at[4], mr.at[4], ctx, zp(i)))
 
-    def gup_step(j, carry):
-        here = ds(j * fw, fw)
-        w[5][:, here] = jnp.dot(hid_t[...], dup[:, here], preferred_element_type=F32).astype(BF16)
-        return carry
-
-    free_w(5)
-    lax.fori_loop(0, ff_w // fw, gup_step, 0)
-    finish()
+    finish(lambda: pass_g(4))
 
     value = lax.dot_general(dattn[...], w[3][...], NT, preferred_element_type=F32)
     dh[...] = value.astype(BF16).reshape(2, seqs, blk, head_w)
     pair = to_owner(2, dh, d_o, False)
-    pass_g(4)
+    send_near(5, 0)
+    send_near(5, 1)
+    send_home(5)
 
     def go_step(j, carry):
         here = ds(j * fw, fw)
@@ -1079,7 +1087,7 @@
     dqkv_st[2] = dv_acc[...].astype(BF16).reshape(2 * chips, blk, HD)
     pair = from_owner(3, dqkv_st, dqkv, True)
 
-    send_g(5)
+    pass_g(5)
     send_g(3)
     arrive(pair)
 
@@ -1133,7 +1141,6 @@
         if i < tps - 1:
             rf_copy(i, off).start()
 
-    pass_g(5)
     pass_g(3)
     for m in range(3):
 
@@ -1223,17 +1230,13 @@
     ff_w = w_gate.shape[1] // 2
     heads = head_w // HD
     slab = width // (2 * chips)
-    ctx = lax.axis_index("ctx")
     frequency = THETA ** (-2.0 * np.arange(HD // 2) / HD)
     frequency = np.concatenate([frequency, frequency])
     starts = np.zeros((blk, 1))
     starts[: 2 * chips, 0] = np.arange(2 * chips) * blk
     inside = np.arange(blk)[:, None] * 1.0
     table = np.stack([f(at * frequency) for at in (starts, inside) for f in (np.cos, np.sin)]).astype(np.float32)
-    gains = jnp.stack([gain_query, gain_key, gain_attention, gain_feedforward]).astype(F32)
-    gains = jnp.pad(gains, ((0, 4), (0, 0)))
-    blank = jnp.zeros_like(gains)
-    gtile = jnp.where(ctx % 2 == 0, jnp.concatenate([gains, blank], axis=1), jnp.concatenate([blank, gains], axis=1))
+    gains = [gain.reshape(1, -1) for gain in (gain_query, gain_key, gain_attention, gain_feedforward)]
     weights = (w_query, w_key, w_value, w_output, w_gate, w_up, w_down)
     dims = (chips, tps, seqs, blk, width, head_w, ff_w)
     halves = (head_w, head_w, head_w, head_w, ff_w, ff_w, ff_w)
@@ -1317,6 +1320,7 @@
         v((both, HD), F32),
         v((both, HD), F32),
         v((8, total), jnp.int32),
+        v((8, 128), F32),
         dma((chips + 1,)),
         dma((2 * chips,)),
     ]
@@ -1329,20 +1333,47 @@
         ]
         + [jax.ShapeDtypeStruct((3,) + weight.shape, BF16) for weight in weights]
         + [jax.ShapeDtypeStruct(weight.shape, BF16) for weight in weights[3:]],
-        in_specs=[hbm] * 9 + [pl.BlockSpec(memory_space=pltpu.SMEM), vmem, vmem],
+        in_specs=[hbm] * 9 + [pl.BlockSpec(memory_space=pltpu.SMEM)] + [vmem] * 5,
         out_specs=[hbm, vmem, vmem] + [hbm] * 11,
         scratch_shapes=scratch,
         compiler_params=pltpu.CompilerParams(
             collective_id=0, has_side_effects=True, vmem_limit_bytes=67043328
         ),
         name="layer",
-    )(tokens.reshape(rows, feats), cotangent.reshape(rows, feats), *weights, block_order, gtile, table)
-    output = results[0].reshape(tokens.shape)
-    grad_input = results[1].reshape(tokens.shape)
-    grads = [jnp.sum(received.astype(F32), axis=0) for received in results[3:6]]
-    grads += [value.astype(F32) for value in results[10:]]
-    lanes = results[2][:, :64]
-    return (output, grad_input, *grads, lanes[2], lanes[3], lanes[0], lanes[1])
+    )(tokens.reshape(rows, feats), cotangent.reshape(rows, feats), *weights, block_order, *gains, table)
+    steps = 8
+    shapes = [value.shape for value in results[:2]] + [weight.shape for weight in weights]
+
+    def rows_of(shape):
+        return pl.BlockSpec((shape[0] // steps, shape[1]), lambda i: (i, 0))
+
+    three = pl.BlockSpec((3, slab // steps, 2 * head_w), lambda i: (0, i, 0))
+    whole = pl.BlockSpec((8, 128), lambda i: (0, 0))
+    gain = pl.BlockSpec((1, 64), lambda i: (0, 0))
+    wide = pl.pallas_call(
+        widen_kernel,
+        grid=(steps,),
+        out_shape=[jax.ShapeDtypeStruct(shape, F32) for shape in shapes] + [jax.ShapeDtypeStruct((1, 64), F32)] * 4,
+        in_specs=[rows_of(shapes[0])] * 2 + [three] * 3 + [rows_of(shape) for shape in shapes[5:]] + [whole],
+        out_specs=[rows_of(shape) for shape in shapes] + [gain] * 4,
+        name="widen",
+    )(*results[:2], *results[3:6], *results[10:], results[2])
+    output = wide[0].reshape(tokens.shape)
+    grad_input = wide[1].reshape(tokens.shape)
+    lanes = [value.reshape(64) for value in wide[9:]]
+    return (output, grad_input, *wide[2:9], lanes[2], lanes[3], lanes[0], lanes[1])
+
+
+def widen_kernel(*refs):
+    given, made = refs[:10], refs[10:]
+    for i in range(2):
+        made[i][...] = given[i][...]
+    for i in range(2, 5):
+        made[i][...] = given[i][0].astype(F32) + given[i][1].astype(F32) + given[i][2].astype(F32)
+    for i in range(5, 9):
+        made[i][...] = given[i][...].astype(F32)
+    for i in range(4):
+        made[9 + i][...] = given[9][i : i + 1, 0:64]
 
 
 def fits(mesh):

time: 374 us -> 345 us (0.922); the launches traced: 369 us -> 344 us
  other arithmetic: 11.1 us -> 0 us
  Pallas kernels: 354 us -> 344 us
    pallas_call x1, Pallas kernels: 354 us -> 335 us  [fused(): pl.pallas_call(functools.partial(layer_kernel, dims), out_shape=[jax.Shap...]
    pallas_call x0 -> x1, Pallas kernels: none -> 8.61 us  [fused(): pl.pallas_call(widen_kernel, grid=(steps,), out_shape=[jax.ShapeDtypeStru...]
    convert_element_type x4 -> x0, other arithmetic: 6.37 us -> none  [fused(): grads += [value.astype(F32) for value in results[10:]]]
where the time goes in v5:
time: 345 us; the launch traced here: 344 us
  Pallas kernels  344 us (100%)
    pallas_call x1, Pallas kernels, fused(): pl.pallas_call(functools.partial(layer_kernel, dims), out_shape=[jax.Shap...  335 us
    pallas_call x1, Pallas kernels, fused(): pl.pallas_call(widen_kernel, grid=(steps,), out_shape=[jax.ShapeDtypeStru...  8.61 us

profile of v5, /device:TPU:0, one launch (start us, length us, event | category | flops | bytes accessed | tf_op | source)
XLA Modules:
  0.0 344.5 jit_solution(13443916504702613726)
XLA Ops:
  0.7 335.0 %layer.1 = (f32[256,512]{1,0:T(8,128)}, f32[256,512]{1,0:T(8,128)}, f32[8,128]{1,0:T(8,128)}, bf16[3,256,512]{2,1,0:T(8,128)(2,1)}, bf16[3,256,512]{2,1,0:T(8,12...) custom-call(bf16[256,512]{1,0:T(8,128)(2,1)} %bitcast.12, ...), custom_call_target="tpu_custom_call" | custom-call | tf_op jit(solution)/shard_map/layer/pallas_call | solution.py:1327
  335.7 8.6 %widen.1 = (f32[256,512]{1,0:T(8,128)}, f32[256,512]{1,0:T(8,128)}, f32[256,512]{1,0:T(8,128)}, f32[256,512]{1,0:T(8,128)}, f32[256,512]{1,0:T(8,128)}, /*index=...) custom-call(f32[256,512]{1,0:T(8,128)} %get-tuple-element.36.refs_0_, ...), custom_call_target="tpu_custom_call" | custom-call | tf_op jit(solution)/shard_map/widen/pallas_call | solution.py:1353

commit v6 on v5

--- a/solution.py
+++ b/solution.py
@@ -938,6 +938,7 @@
     def down_ready(i):
         if i == 0:
             w_own[6].wait()
+        if i == 1:
             pass_w(6)
         got_w(6, *((4,), (0, 1), (2, 3), (5, 6))[i])
 
@@ -1341,7 +1342,7 @@
         ),
         name="layer",
     )(tokens.reshape(rows, feats), cotangent.reshape(rows, feats), *weights, block_order, *gains, table)
-    steps = 8
+    steps = 2
     shapes = [value.shape for value in results[:2]] + [weight.shape for weight in weights]
 
     def rows_of(shape):

time: 345 us -> 338 us (0.980)
  Pallas kernels: 344 us -> 337 us
    pallas_call x1, Pallas kernels: 335 us -> 331 us  [fused(): pl.pallas_call(functools.partial(layer_kernel, dims), out_shape=[jax.Shap...]
where the time goes in v6:
time: 338 us
  Pallas kernels  337 us (100%)
    pallas_call x1, Pallas kernels, fused(): pl.pallas_call(functools.partial(layer_kernel, dims), out_shape=[jax.Shap...  331 us

profile of v6, /device:TPU:0, one launch (start us, length us, event | category | flops | bytes accessed | tf_op | source)
XLA Modules:
  0.0 337.9 jit_solution(7583914512720471779)
XLA Ops:
  0.7 331.3 %layer.1 = (f32[256,512]{1,0:T(8,128)}, f32[256,512]{1,0:T(8,128)}, f32[8,128]{1,0:T(8,128)}, bf16[3,256,512]{2,1,0:T(8,128)(2,1)}, bf16[3,256,512]{2,1,0:T(8,12...) custom-call(bf16[256,512]{1,0:T(8,128)(2,1)} %bitcast.12, ...), custom_call_target="tpu_custom_call" | custom-call | tf_op jit(solution)/shard_map/layer/pallas_call | solution.py:1328
  331.9 5.8 %widen.1 = (f32[256,512]{1,0:T(8,128)}, f32[256,512]{1,0:T(8,128)}, f32[256,512]{1,0:T(8,128)}, f32[256,512]{1,0:T(8,128)}, f32[256,512]{1,0:T(8,128)}, /*index=...) custom-call(f32[256,512]{1,0:T(8,128)} %get-tuple-element.36.refs_0_, ...), custom_call_target="tpu_custom_call" | custom-call | tf_op jit(solution)/shard_map/widen/pallas_call | solution.py:1354
